TPU v7x, 32 devices: a whole 2x2x4 slice. The times are simulated.
32 devices in a mesh: grp: 16 (over z, x, core), fsdp: 2 (over y).
Axes of the slice: x: 2, y: 2, z: 4, core: 2. Of those that a mesh axis runs over, the one named last changes fastest.
Arguments:
- tokens: bfloat16 [12288, 3584], P(('grp', 'fsdp')), may hold values from -6 to 6
- target: bfloat16 [12288, 1024], P(('grp', 'fsdp')), may hold values from -6 to 6
- weight: bfloat16 [3584, 1024], P('fsdp'), may hold values from -0.09375 to 0.09375
- factor_a: bfloat16 [3584, 512], P('fsdp'), may hold values from -6 to 6
- factor_b: bfloat16 [512, 1024], replicated, may hold values from -6 to 6
- counts: int32 [256], replicated, may hold values from 1 to 192, 12288 in all
- cand_index: int32 [256, 2], replicated, may hold values from 0 to 511
Outputs:
- update: float32 [3584, 1024], P('fsdp')
- scores: float32 [256], replicated
Inputs may be any that keep to these rules, and one draw needn't show every extreme that they name: The counts sum to 12288; candidate i owns the tokens from counts[0] + ... + counts[i-1] on.
All inputs are finite; a program needn't handle non-finite values.
Results may differ from a plain program's by a relative error of at most 0.003.
Values may be sent and summed in bfloat16 or wider, within the bound.
No kernel may reach another device: no remote copies, remote signals or barrier semaphores. Data moves between devices by JAX's collectives and lax.ppermute only.
A program may use at most 64 MiB of HBM per device.

v0:
```python
import jax
import jax.numpy as jnp
from jax import lax
from jax.sharding import PartitionSpec as P

D = 3584


def per_device(tokens, target, weight, factor_a, factor_b, counts, cand_index):
    rows = tokens.shape[0]
    width_out = weight.shape[1]
    pool_size = factor_a.shape[1]
    total_cands = counts.shape[0]
    noise = 0.5 * D ** (-0.5)
    spread_rows = lax.all_to_all(tokens, "fsdp", split_axis=1, concat_axis=0, tiled=True)
    joined = jnp.concatenate((weight, factor_a), axis=1)
    summed = lax.psum_scatter(
        jnp.dot(spread_rows, joined, preferred_element_type=jnp.float32),
        "fsdp",
        scatter_dimension=0,
        tiled=True,
    )
    base = summed[:, :width_out]
    pool_scores = summed[:, width_out:]
    ends = jnp.cumsum(counts)
    position = lax.axis_index(("grp", "fsdp")) * rows + jnp.arange(rows, dtype=jnp.int32)
    owner = jnp.sum((ends[None, :] <= position[:, None]).astype(jnp.int32), axis=1)
    left_index = cand_index[:, 0]
    right_index = cand_index[:, 1]
    tok_a = jnp.take(left_index, owner)
    tok_b = jnp.take(right_index, owner)
    pool_ids = jnp.arange(pool_size, dtype=jnp.int32)
    picked = jnp.sum(jnp.where(tok_a[:, None] == pool_ids[None, :], pool_scores, 0.0), axis=1)
    right_rows = jnp.take(factor_b, tok_b, axis=0).astype(jnp.float32)
    output = base + noise * picked[:, None] * right_rows
    diff = output - target.astype(jnp.float32)
    loss = jnp.mean(diff * diff, axis=1)
    cand_ids = jnp.arange(total_cands, dtype=jnp.int32)
    partial_value = jnp.sum(
        jnp.where(owner[:, None] == cand_ids[None, :], loss[:, None], 0.0), axis=0
    )
    totals = lax.psum(partial_value, ("grp", "fsdp"))
    fitness = -totals / counts.astype(jnp.float32)
    middle = jnp.mean(fitness)
    variance = jnp.mean((fitness - middle) ** 2)
    scores = (fitness - middle) / jnp.sqrt(variance + 1e-06)
    selector = (pool_ids[:, None] == left_index[None, :]).astype(jnp.bfloat16)
    columns = jnp.dot(factor_a, selector, preferred_element_type=jnp.float32)
    scaled = (columns * scores[None, :]).astype(jnp.bfloat16)
    chosen_rows = jnp.take(factor_b, right_index, axis=0)
    summed_update = jnp.dot(scaled, chosen_rows, preferred_element_type=jnp.float32)
    update = summed_update / jnp.sqrt(jnp.float32(total_cands))
    return (update, scores)


def solution(mesh):
    in_specs = (
        P(("grp", "fsdp"), None),
        P(("grp", "fsdp"), None),
        P("fsdp", None),
        P("fsdp", None),
        P(),
        P(),
        P(),
    )
    out_specs = (P("fsdp", None), P())
    return jax.shard_map(
        per_device, mesh=mesh, in_specs=in_specs, out_specs=out_specs, check_vma=False
    )
```

profile of v0, /device:TPU:0, one launch (start us, length us, event | category | flops | bytes accessed | tf_op | source)
XLA Modules:
  0.0 185.1 jit_solution(5749809767784370416)
XLA Ops:
  7.2 4.6 %copy.17 = bf16[384,3584]{0,1:T(8,128)(2,1)} copy(bf16[384,3584]{1,0:T(8,128)(2,1)} %param.9) | data formatting | bytes 5505024 | tf_op args[0]
  11.8 39.5 %all_to_all.19 = bf16[384,2,1792]{0,2,1:T(8,128)(2,1)} all-to-all(bf16[384,2,1792]{0,2,1:T(8,128)(2,1)} %bitcast.17), channel_id=1, replica_groups=mesh['grp'=16,'fsdp'=2] {'fsdp'}, dimensions={1} | all-to-all | bytes 5505024 | tf_op jit(solution)/shard_map/all_to_all | solution.py:15
  51.3 4.8 %copy.18 = bf16[2,384,1792]{2,1,0:T(8,128)(2,1)} copy(bf16[2,384,1792]{1,2,0:T(8,128)(2,1)} %bitcast.16) | data formatting | bytes 5505024 | tf_op jit(solution)/shard_map/all_to_all | solution.py:15
  56.1 9.6 %fusion.4 = f32[768,1536]{0,1:T(8,128)} fusion(bf16[768,1792]{1,0:T(8,128)(2,1)} %bitcast.18, bf16[1792,512]{1,0:T(8,128)(2,1)S(1)} %copy-done.1, bf16[1792,1024]{1,0:T(8,128)(2,1)} %param.11), kind=kOutput, calls=%fused_computation.9 | convolution fusion | flops 4238868480 | bytes 12976128 | tf_op jit(solution)/shard_map/dot_general | solution.py:18
  65.7 0.6 copy-done.4
  66.4 0.3 reduce-window.9
  66.7 0.1 slice.20
  66.8 0.1 slice_reduce_fusion
  66.9 0.1 add_bitcast_fusion
  67.0 0.2 convert_reduce_fusion
  67.3 2.8 %gather_fusion.2 = s32[384]{0:T(512)S(1)} fusion(s32[256]{0:T(256)S(1)} %bitcast.13, s32[1024]{0:T(1024)S(1)} %pad_clamp_fusion.2), kind=kCustom, calls=%fused_computation.clone | custom fusion | bytes 4608 | tf_op jit(solution)/shard_map/jit(_take)/gather | solution.py:30
  70.1 2.8 %gather_fusion.3 = s32[384]{0:T(512)S(1)} fusion(s32[256]{0:T(256)S(1)} %bitcast.15, s32[1024]{0:T(1024)S(1)} %pad_clamp_fusion.2), kind=kCustom, calls=%fused_computation.1.clone | custom fusion | bytes 4608 | tf_op jit(solution)/shard_map/jit(_take)/gather | solution.py:31
  73.0 2.1 %gather_fusion = bf16[384,1024]{1,0:T(8,128)(2,1)S(1)} fusion(bf16[512,1024]{1,0:T(8,128)(2,1)S(1)} %copy-done, s32[1024]{0:T(1024)S(1)} %pad_clamp_fusion.1), kind=kCustom, calls=%fused_computation.2 | custom fusion | bytes 1574400 | tf_op jit(solution)/shard_map/jit(_take)/gather | solution.py:34
  75.0 0.4 copy.19
  75.4 0.4 copy.20
  75.8 1.2 gather_fusion.1
  77.0 49.5 %reduce-scatter.2.cloned.1.call-done = f32[384,1536]{0,1:T(8,128)} async-done(((f32[768,1536]{0,1:T(8,128)}), f32[384,1536]{0,1:T(8,128)}) %reduce-scatter.2.cloned.1.call-update) | async-done | bytes 2359312 | tf_op jit(solution)/shard_map/reduce_scatter | solution.py:17
  126.5 1.3 fusion.12
  127.7 1.9 fusion.10
  129.6 0.2 select_reduce_fusion
  129.8 39.5 %psum.7 = f32[256]{0:T(256)S(1)} all-reduce(f32[256]{0:T(256)S(1)} %select_reduce_fusion), channel_id=1, replica_groups=mesh['grp'=16,'fsdp'=2] {'grp','fsdp'}, use_global_device_ids=true, to_apply=%region_7.9 | all-reduce | flops 256 | bytes 2048 | tf_op jit(solution)/shard_map/psum | solution.py:42
  169.3 0.6 fusion.23
  170.5 0.6 multiply_reduce_fusion
  171.9 6.4 %convolution_multiply_fusion = f32[1792,1024]{1,0:T(8,128)} fusion(bf16[1792,512]{1,0:T(8,128)(2,1)} %param.12, f32[256]{0:T(256)S(1)} %subtract_divide_fusion, bf16[256,1024]{1,0:T(8,128)(2,1)S(1)} %gather_fusion.1, pred[256]{0:T(512)(128)(4,1)S(1)} %get-tuple-element.3, s32[256]{0:T(256)S(1)} %bitcast.14), kind=kOutput, calls=%fused_computation.8 | convolution fusion | flops 1412562944 | bytes 9701632 | tf_op jit(solution)/shard_map/dot_general | solution.py:51
  (26 shorter events, 0.2 us)
Async XLA Ops:
  7.2 65.8 %copy-start = (bf16[512,1024]{1,0:T(8,128)(2,1)S(1)}, bf16[512,1024]{1,0:T(8,128)(2,1)}, u32[]{:S(2)}) copy-start(bf16[512,1024]{1,0:T(8,128)(2,1)} %param.13) | copy-start | bytes 3145732
  7.2 119.3 %reduce-scatter.2.cloned.1.call-start = ((), (), s32[]{:S(2)}) async-start(), calls=%async_computation.2 | async-start | bytes 7077888 | tf_op jit(solution)/shard_map/reduce_scatter | solution.py:17
  51.3 4.8 %copy-start.1 = (bf16[1792,512]{1,0:T(8,128)(2,1)S(1)}, bf16[1792,512]{1,0:T(8,128)(2,1)}, u32[]{:S(2)}) copy-start(bf16[1792,512]{1,0:T(8,128)(2,1)} %param.12) | copy-start | bytes 5505028
  65.7 0.7 copy-start.4
  65.7 1.5 copy-start.3
  72.9 2.5 %copy-start.2 = (bf16[384,1024]{1,0:T(8,128)(2,1)S(1)}, bf16[384,1024]{1,0:T(8,128)(2,1)}, u32[]{:S(2)}) copy-start(bf16[384,1024]{1,0:T(8,128)(2,1)} %param.10) | copy-start | bytes 2359300
  171.8 6.4 %copy-start.5 = (f32[256]{0:T(256)}, f32[256]{0:T(256)S(1)}, u32[]{:S(2)}) copy-start(f32[256]{0:T(256)S(1)} %subtract_divide_fusion) | copy-start | bytes 3076
Sparse Core Ops, SparseCore 0:
  65.9 60.5 reduce-scatter.1
where the time goes:
time: 186 us; the launch traced here: 185 us
  blocking collectives  79 us (42%)
  waiting for transfers between devices  49.5 us (27%)
  local copies, waits for them, and re-layouts  19.8 us (11%)
  matrix products  16 us (9%)
  between operations  15.5 us (8%)
  other arithmetic  5.24 us (3%)
    reduce_scatter x1, waiting for transfers between devices, per_device(): lax.psum_scatter(jnp.dot(spread_rows, joined, preferred_element_type=jnp....  49.5 us
    all_to_all x1, blocking collectives, per_device(): lax.all_to_all(tokens, 'fsdp', split_axis=1, concat_axis=0, tiled=True)  39.5 us
    psum x1, blocking collectives, per_device(): totals = lax.psum(partial_value, ('grp', 'fsdp'))  39.5 us
    dot_general x1, matrix products, per_device(): jnp.dot(spread_rows, joined, preferred_element_type=jnp.float32)  9.63 us
    dot_general x1, matrix products, per_device(): jnp.dot(scaled, chosen_rows, preferred_element_type=jnp.float32)  6.42 us
    unnamed x14, local copies, waits for them, and re-layouts  5.6 us
    all_to_all x1, local copies, waits for them, and re-layouts, per_device(): lax.all_to_all(tokens, 'fsdp', split_axis=1, concat_axis=0, tiled=True)  4.77 us
  transfers between devices with their start and end apart: 1, of which 1 were waited for; matrix products, arithmetic and copies ran while one was open for 6% of the time, Pallas kernels for 0%

commit v1 on v0

v1 whole, which is shorter than its diff:
```python
import functools

import jax
import jax.numpy as jnp
from jax import lax
from jax.experimental import pallas as pl
from jax.experimental.pallas import tpu as pltpu
from jax.sharding import PartitionSpec as P


AXES = ("grp", "fsdp")
f32 = jnp.float32
bf16 = jnp.bfloat16
PIECES = 8


def turned(row, height):
    return jnp.transpose(jnp.broadcast_to(row.astype(f32), (height, row.shape[1])))


def matches(row, pool):
    ids = lax.broadcasted_iota(jnp.int32, (pool, row.shape[1]), 0)
    return (ids == row).astype(f32).astype(bf16)


def pack_kernel(order, index_ref, weight_ref, factor_ref, *refs):
    outs, factors, w_sem, a_sem = refs[:-3], refs[-3], refs[-2], refs[-1]
    height, width = outs[0].shape[0], weight_ref.shape[1]
    copies = []
    for k, (out, block) in enumerate(zip(outs, order())):
        rows = pl.ds(pl.multiple_of(block * height, 16), height)
        a = pltpu.make_async_copy(factor_ref.at[rows], factors.at[k], a_sem.at[k])
        w = pltpu.make_async_copy(weight_ref.at[rows], out.at[:, pl.ds(0, width)], w_sem.at[k])
        a.start()
        w.start()
        copies.append((a, w))
    selector = matches(index_ref[0:1, :], factor_ref.shape[1])
    for k, (out, (a, w)) in enumerate(zip(outs, copies)):
        a.wait()
        out[:, width:] = jnp.dot(factors[k], selector, preferred_element_type=f32).astype(bf16)
    for _, w in copies:
        w.wait()


def vmem():
    return pl.BlockSpec(memory_space=pltpu.VMEM)


def hbm():
    return pl.BlockSpec(memory_space=pltpu.HBM)


def in_hbm(*arrays):
    return [pltpu.with_memory_space_constraint(a, pltpu.HBM) for a in arrays]


def params(mib):
    return pltpu.CompilerParams(vmem_limit_bytes=mib << 20)


def pack(order, count, index, weight, factor_a, height):
    width, pool, cands = weight.shape[1], factor_a.shape[1], index.shape[1]
    return pl.pallas_call(
        functools.partial(pack_kernel, order),
        in_specs=[vmem(), hbm(), hbm()],
        out_specs=[vmem()] * count,
        out_shape=[jax.ShapeDtypeStruct((height, width + cands), bf16)] * count,
        scratch_shapes=[
            pltpu.VMEM((count, height, pool), bf16),
            pltpu.SemaphoreType.DMA((count,)),
            pltpu.SemaphoreType.DMA((count,)),
        ],
        compiler_params=params(8),
        name="pack",
    )(index, *in_hbm(weight, factor_a))


def near_kernel(
    index_ref, counts_ref, tokens_ref, weight_ref, factor_ref, rights_ref, target_ref,
    far_ref, base_ref, sc_ref, hot_ref, right_ref, columns_ref, chosen_ref,
    x, w, a, b, t, sem,
):
    fsdp = lax.axis_index("fsdp")
    device = lax.axis_index("grp") * lax.axis_size("fsdp") + fsdp
    rows, depth = far_ref.shape
    cands = counts_ref.shape[1]
    pool = factor_ref.shape[1]
    near = pl.ds(pl.multiple_of(fsdp * depth, 128), depth)
    other = pl.ds(pl.multiple_of((1 - fsdp) * depth, 128), depth)
    pairs = [
        (factor_ref, a), (rights_ref, b), (tokens_ref.at[:, near], x), (weight_ref, w),
        (target_ref, t), (tokens_ref.at[:, other], far_ref),
    ]
    copies = [pltpu.make_async_copy(s, d, sem.at[k]) for k, (s, d) in enumerate(pairs)]
    for c in copies:
        c.start()
    along = lax.broadcasted_iota(jnp.int32, (cands, cands), 0)
    across = lax.broadcasted_iota(jnp.int32, (cands, cands), 1)
    ends = jnp.sum(jnp.where(along <= across, turned(counts_ref[...], cands), 0.0), axis=0, keepdims=True)
    begins = ends - counts_ref[...].astype(f32)
    position = (device * rows + lax.broadcasted_iota(jnp.int32, (rows, cands), 0)).astype(f32)
    hot = jnp.where((position >= begins) & (position < ends), 1.0, 0.0).astype(bf16)
    hot_ref[...] = hot
    copies[0].wait()
    columns_ref[...] = jnp.dot(a[...], matches(index_ref[0:1, :], pool), preferred_element_type=f32).astype(bf16)
    copies[1].wait()
    chosen = lax.dot_general(
        matches(index_ref[1:2, :], pool), b[...], (((0,), (0,)), ((), ())), preferred_element_type=f32
    ).astype(bf16)
    chosen_ref[...] = chosen
    right_ref[...] = jnp.dot(hot, chosen, preferred_element_type=f32).astype(bf16)
    copies[2].wait()
    sc_ref[...] = jnp.dot(x[...], columns_ref[...], preferred_element_type=f32)
    copies[3].wait()
    copies[4].wait()
    base_ref[...] = jnp.dot(x[...], w[...], preferred_element_type=f32) - t[...].astype(f32)
    copies[5].wait()


def near_half(index, counts, tokens, weight, factor_a, factor_b, target):
    rows, width = target.shape
    depth, cands, pool = weight.shape[0], counts.shape[1], factor_a.shape[1]

    def shaped(*shape, dtype=bf16):
        return jax.ShapeDtypeStruct(shape, dtype)

    return pl.pallas_call(
        near_kernel,
        in_specs=[vmem(), vmem()] + [hbm()] * 5,
        out_specs=[vmem()] * 7,
        out_shape=[
            shaped(rows, depth), shaped(rows, width, dtype=f32), shaped(rows, cands, dtype=f32),
            shaped(rows, cands), shaped(rows, width), shaped(depth, cands), shaped(cands, width),
        ],
        scratch_shapes=[
            pltpu.VMEM((rows, depth), bf16), pltpu.VMEM((depth, width), bf16), pltpu.VMEM((depth, pool), bf16),
            pltpu.VMEM((pool, width), bf16), pltpu.VMEM((rows, width), bf16), pltpu.SemaphoreType.DMA((6,)),
        ],
        compiler_params=params(28),
        cost_estimate=pl.CostEstimate(
            flops=2 * rows * depth * (width + cands) * 4, bytes_accessed=12 << 20, transcendentals=0
        ),
        name="near",
    )(index, counts, *in_hbm(tokens, weight, factor_a, factor_b, target))


def loss_kernel(noise, order, x_ref, base_ref, sc_ref, right_ref, hot_ref, *refs):
    pieces, out_ref, held = refs[:-2], refs[-2], refs[-1]
    height = pieces[0].shape[0]
    for piece, block in zip(pieces, order()):
        held[pl.ds(pl.multiple_of(block * height, 16), height), :] = piece[...]
    rows, width = base_ref.shape
    total = None
    step = 128
    for r in range(0, rows, step):
        s = slice(r, r + step)
        acc = jnp.dot(x_ref[s, :], held[...], preferred_element_type=f32)
        hot = hot_ref[s, :].astype(f32)
        picked = jnp.sum(hot * (acc[:, width:] + sc_ref[s, :]), axis=1, keepdims=True) * noise
        diff = acc[:, :width] + base_ref[s, :] + picked * right_ref[s, :].astype(f32)
        loss = jnp.sum(diff * diff, axis=1, keepdims=True) * (1.0 / width)
        part = jnp.sum(hot * loss, axis=0, keepdims=True)
        total = part if total is None else total + part
    out_ref[...] = jnp.broadcast_to(total[None], out_ref.shape)


def losses(noise, order, x, base, sc, right, hot, pieces, devices):
    depth, width, cands = x.shape[1], base.shape[1], hot.shape[1]
    return pl.pallas_call(
        functools.partial(loss_kernel, noise, order),
        in_specs=[vmem()] * (5 + len(pieces)),
        out_specs=vmem(),
        out_shape=jax.ShapeDtypeStruct((devices, 1, cands), f32),
        scratch_shapes=[pltpu.VMEM((depth, width + cands), bf16)],
        compiler_params=params(20),
        name="losses",
    )(x, base, sc, right, hot, *pieces)


def update_kernel(step, parts_ref, counts_ref, columns_ref, chosen_ref, update_ref, scores_ref, held, sem):
    cands = counts_ref.shape[1]
    totals = jnp.sum(parts_ref[...], axis=0)
    fitness = -totals / counts_ref[...].astype(f32)
    middle = jnp.sum(fitness, axis=1, keepdims=True) / cands
    spread = jnp.sum((fitness - middle) ** 2, axis=1, keepdims=True) / cands
    scores = (fitness - middle) / jnp.sqrt(spread + 1e-06)
    scores_ref[...] = scores
    copies = []
    for k in range(columns_ref.shape[0] // step):
        s = pl.ds(k * step, step)
        scaled = (columns_ref[s, :].astype(f32) * scores).astype(bf16)
        held[s, :] = jnp.dot(scaled, chosen_ref[...], preferred_element_type=f32) * (1.0 / cands**0.5)
        c = pltpu.make_async_copy(held.at[s], update_ref.at[s], sem.at[k])
        c.start()
        copies.append(c)
    for c in copies:
        c.wait()


def update_of(parts, counts, columns, chosen):
    depth, cands = columns.shape
    width = chosen.shape[1]
    step = next(s for s in (128, 64, 32, 16, depth) if depth % s == 0)
    return pl.pallas_call(
        functools.partial(update_kernel, step),
        in_specs=[vmem()] * 4,
        out_specs=[hbm(), vmem()],
        out_shape=[jax.ShapeDtypeStruct((depth, width), f32), jax.ShapeDtypeStruct((1, cands), f32)],
        scratch_shapes=[pltpu.VMEM((depth, width), f32), pltpu.SemaphoreType.DMA((depth // step,))],
        compiler_params=params(20),
        name="update",
    )(parts, counts, columns, chosen)


def hop(value, bit, devices):
    return lax.ppermute(value, AXES, [(i, i ^ bit) for i in range(devices)])


def place():
    grp = lax.axis_index("grp")
    return jnp.bitwise_and(grp, 1), jnp.bitwise_and(jnp.right_shift(grp, 1), 3)


def sent():
    core, spot = place()
    return [2 * i + core for i in (spot, spot + 4, 3 - spot, 7 - spot)]


def arrived():
    core, spot = place()
    x, z = jnp.bitwise_xor(spot, 1), jnp.bitwise_xor(spot, 2)
    ids = [spot, spot + 4, x, z, 3 - spot, 7 - spot, x + 4, z + 4]
    return [2 * i + core for i in ids] + [2 * i + 1 - core for i in ids]


def per_device(groups, parts, tokens, target, weight, factor_a, factor_b, counts, cand_index):
    return compute(groups, parts, tokens, target, weight, factor_a, factor_b, counts, cand_index)


def compute(groups, parts, tokens, target, weight, factor_a, factor_b, counts, cand_index):
    devices = groups * parts
    rows, full = tokens.shape
    depth = weight.shape[0]
    cands = counts.shape[0]
    noise = 0.5 * full ** (-0.5)
    index = cand_index.T
    if parts == 2 and groups % 8 == 0 and depth % (2 * PIECES * 16) == 0:
        height = depth // (2 * PIECES)
        first, second, third, fourth = pack(sent, 4, index, weight, factor_a, height)
        y1, y2 = hop(first, 1, devices), hop(second, 1, devices)
        y3, y4 = hop(third, 1, devices), hop(fourth, 1, devices)
        x1, z1 = hop(y1, 4, devices), hop(y1, 8, devices)
        x2, z2 = hop(y2, 4, devices), hop(y2, 8, devices)
        own = [y1, y2, x1, z1, y3, y4, x2, z2]
        swapped = [hop(v, 2, devices) for v in own]
        far, base, sc, hot, right_rows, columns, chosen = near_half(
            index, counts[None, :], tokens, weight, factor_a, factor_b, target
        )
        sums = losses(noise, arrived, far, base, sc, right_rows, hot, own + swapped, devices)
    else:
        left, right = cand_index[:, 0], cand_index[:, 1]
        cand_ids = jnp.arange(cands, dtype=jnp.int32)
        ends = jnp.sum(jnp.where(cand_ids[:, None] <= cand_ids[None, :], counts[:, None], 0), axis=0)
        position = lax.axis_index(AXES) * rows + jnp.arange(rows, dtype=jnp.int32)
        hot = (position[:, None] >= (ends - counts)[None, :]) & (position[:, None] < ends[None, :])
        owned = hot.astype(f32)
        columns = jnp.take(factor_a, left, axis=1)
        chosen = jnp.take(factor_b, right, axis=0)
        right_rows = jnp.dot(hot.astype(bf16), chosen, preferred_element_type=f32)
        all_weight = lax.all_gather(weight, "fsdp", axis=0, tiled=True)
        all_columns = lax.all_gather(columns, "fsdp", axis=0, tiled=True)
        base = jnp.dot(tokens, all_weight, preferred_element_type=f32)
        sc = jnp.dot(tokens, all_columns, preferred_element_type=f32)
        picked = noise * jnp.sum(owned * sc, axis=1)
        diff = base + picked[:, None] * right_rows - target.astype(f32)
        loss = jnp.mean(diff * diff, axis=1)
        sums = jnp.broadcast_to(jnp.sum(owned * loss[:, None], axis=0)[None, None, :], (devices, 1, cands))
    spread = lax.all_to_all(sums, AXES, split_axis=0, concat_axis=0, tiled=True)
    update, scores = update_of(spread, counts[None, :], columns, chosen)
    return update, scores[0]


def solution(mesh):
    in_specs = (
        P(AXES, None),
        P(AXES, None),
        P("fsdp", None),
        P("fsdp", None),
        P(),
        P(),
        P(),
    )
    return jax.shard_map(
        functools.partial(per_device, mesh.shape["grp"], mesh.shape["fsdp"]),
        mesh=mesh,
        in_specs=in_specs,
        out_specs=(P("fsdp", None), P()),
        check_vma=False,
    )
```

time: 186 us -> 66.3 us (0.36)
  blocking collectives: 79 us -> 12 us
  waiting for transfers between devices: 49.5 us -> 24.5 us
  local copies, waits for them, and re-layouts: 19.8 us -> 0.68 us
  matrix products: 16 us -> 0 us
  between operations: 15.5 us -> 0.72 us
  Pallas kernels: 0 us -> 14.7 us
  starting transfers between devices: 0.04 us -> 13.6 us
  other arithmetic: 5.24 us -> 0 us
    reduce_scatter x1 -> x0, waiting for transfers between devices: 49.5 us -> none  [per_device(): lax.psum_scatter(jnp.dot(spread_rows, joined, preferred_element_type=jnp....]
    psum x1 -> x0, blocking collectives: 39.5 us -> none  [per_device(): totals = lax.psum(partial_value, ('grp', 'fsdp'))]
    all_to_all x1, blocking collectives: 39.5 us -> 12 us  [compute(): spread = lax.all_to_all(sums, AXES, split_axis=0, concat_axis=0, tiled=True)]
    ppermute x0 -> x16, waiting for transfers between devices: none -> 24.5 us  [hop(): return lax.ppermute(value, AXES, [(i, i ^ bit) for i in range(devices)])]
    dot_general x2 -> x0, matrix products: 16 us -> none  [the longest x1 9.63 us: per_device(): jnp.dot(spread_rows, joined, preferred_element_type=jnp.float32)]
    pallas_call x0 -> x4, Pallas kernels: none -> 14.7 us  [the longest x1 5.89 us: near_half(): pl.pallas_call(near_kernel, in_specs=[vmem(), vmem()] + [hbm()] * 5, out_...]
    ppermute x0 -> x16, starting transfers between devices: none -> 13.6 us  [hop(): return lax.ppermute(value, AXES, [(i, i ^ bit) for i in range(devices)])]
    gather x5 -> x0, local copies, waits for them, and re-layouts: 9.21 us -> none  [the longest x1 2.81 us: per_device(): tok_a = jnp.take(left_index, owner)]
  transfers between devices with their start and end apart: 1 -> 16, of which waited for: 1 -> 6; matrix products, arithmetic and copies ran while one was open for 6% -> 0% of each run, Pallas kernels for 0% -> 9%
where the time goes in v1:
time: 66.3 us; the launch traced here: 66.1 us
  waiting for transfers between devices  24.5 us (37%)
  Pallas kernels  14.7 us (22%)
  starting transfers between devices  13.6 us (21%)
  blocking collectives  12 us (18%)
  between operations  0.72 us (1%)
  local copies, waits for them, and re-layouts  0.68 us (1%)
    ppermute x16, waiting for transfers between devices, hop(): return lax.ppermute(value, AXES, [(i, i ^ bit) for i in range(devices)])  24.5 us
    ppermute x16, starting transfers between devices, hop(): return lax.ppermute(value, AXES, [(i, i ^ bit) for i in range(devices)])  13.6 us
    all_to_all x1, blocking collectives, compute(): spread = lax.all_to_all(sums, AXES, split_axis=0, concat_axis=0, tiled=True)  12 us
    pallas_call x1, Pallas kernels, near_half(): pl.pallas_call(near_kernel, in_specs=[vmem(), vmem()] + [hbm()] * 5, out_...  5.89 us
    pallas_call x1, Pallas kernels, update_of(): pl.pallas_call(functools.partial(update_kernel, step), in_specs=[vmem()]...  4.07 us
    pallas_call x1, Pallas kernels, losses(): pl.pallas_call(functools.partial(loss_kernel, noise, order), in_specs=[vm...  2.87 us
    pallas_call x1, Pallas kernels, pack(): pl.pallas_call(functools.partial(pack_kernel, order), in_specs=[vmem(), h...  1.84 us
  transfers between devices with their start and end apart: 16, of which 6 were waited for; matrix products, arithmetic and copies ran while one was open for 0% of the time, Pallas kernels for 9%

profile of v1, /device:TPU:0, one launch (start us, length us, event | category | flops | bytes accessed | tf_op | source)
XLA Modules:
  0.0 66.1 jit_solution(529046317484901321)
XLA Ops:
  0.6 0.7 %copy-done = s32[256,2]{0,1:T(2,128)S(1)} copy-done((s32[256,2]{0,1:T(2,128)S(1)}, s32[256,2]{0,1:T(2,128)}, u32[]{:S(2)}) %copy-start) | copy-done | bytes 2072
  1.3 1.8 %pack.1 = (bf16[112,1280]{1,0:T(8,128)(2,1)S(1)}, bf16[112,1280]{1,0:T(8,128)(2,1)S(1)}, bf16[112,1280]{1,0:T(8,128)(2,1)S(1)}, bf16[112,1280]{1,0:T(8,128)(2,1)S(1)}) custom-call(s32[2,256]{1,0:T(2,128)S(1)} %bitcast.3, bf16[1792,1024]{1,0:T(8,128)(2,1)} %weight_ref.3, bf16[1792,512]{1,0:T(8,128)(2,1)} %factor_ref.3), custom_call_target="tpu_custom_call" | custom-call | tf_op jit(solution)/shard_map/pack/pallas_call | solution.py:63
  3.2 3.1 %collective-permute-start = (bf16[112,1280]{1,0:T(8,128)(2,1)S(1)}, bf16[112,1280]{1,0:T(8,128)(2,1)S(1)}, u32[]{:S(2)}, u32[]{:S(2)}) collective-permute-start(bf16[112,1280]{1,0:T(8,128)(2,1)S(1)} %get-tuple-element.20), channel_id=1, source_target_pairs={{0,1},{1,0},{2,3},{3,2},{4,5},{5,4},{6,7},{7,6},{8,9},{9,8},{10,11... | collective-permute-start | bytes 860168 | tf_op jit(solution)/shard_map/ppermute | solution.py:216
  6.2 0.1 collective-permute-start.1
  6.3 1.9 %collective-permute-start.4 = (bf16[112,1280]{1,0:T(8,128)(2,1)S(1)}, bf16[112,1280]{1,0:T(8,128)(2,1)S(1)}, u32[]{:S(2)}, u32[]{:S(2)}) collective-permute-start(bf16[112,1280]{1,0:T(8,128)(2,1)S(1)} %get-tuple-element.22), channel_id=1, source_target_pairs={{0,1},{1,0},{2,3},{3,2},{4,5},{5,4},{6,7},{7,6},{8,9},{9,8},{10,11... | collective-permute-start | bytes 860168 | tf_op jit(solution)/shard_map/ppermute | solution.py:216
  8.3 0.1 collective-permute-start.5
  8.3 5.6 %collective-permute-done.refs_0_ = bf16[112,1280]{1,0:T(8,128)(2,1)S(1)} collective-permute-done((bf16[112,1280]{1,0:T(8,128)(2,1)S(1)}, bf16[112,1280]{1,0:T(8,128)(2,1)S(1)}, u32[]{:S(2)}, u32[]{:S(2)}) %collective-permute-start) | collective-permute-done | bytes 286752 | tf_op jit(solution)/shard_map/ppermute | solution.py:216
  13.9 0.0 collective-permute-start.8
  13.9 2.1 %collective-permute-start.3 = (bf16[112,1280]{1,0:T(8,128)(2,1)S(1)}, bf16[112,1280]{1,0:T(8,128)(2,1)S(1)}, u32[]{:S(2)}, u32[]{:S(2)}) collective-permute-start(bf16[112,1280]{1,0:T(8,128)(2,1)S(1)} %collective-permute-done.refs_0_), channel_id=1, source_target_pairs={{0,8},{1,9},{2,10},{3,11},{4,12},{5,13},{6,14},{7,15},{8,0},{9,1},... | collective-permute-start | bytes 860168 | tf_op jit(solution)/shard_map/ppermute | solution.py:216
  16.0 4.1 %collective-permute-done.1.refs_1_ = bf16[112,1280]{1,0:T(8,128)(2,1)S(1)} collective-permute-done((bf16[112,1280]{1,0:T(8,128)(2,1)S(1)}, bf16[112,1280]{1,0:T(8,128)(2,1)S(1)}, u32[]{:S(2)}, u32[]{:S(2)}) %collective-permute-start.1) | collective-permute-done | bytes 286752 | tf_op jit(solution)/shard_map/ppermute | solution.py:216
  20.1 2.0 %collective-permute-start.2 = (bf16[112,1280]{1,0:T(8,128)(2,1)S(1)}, bf16[112,1280]{1,0:T(8,128)(2,1)S(1)}, u32[]{:S(2)}, u32[]{:S(2)}) collective-permute-start(bf16[112,1280]{1,0:T(8,128)(2,1)S(1)} %collective-permute-done.refs_0_), channel_id=1, source_target_pairs={{0,4},{1,5},{2,6},{3,7},{4,0},{5,1},{6,2},{7,3},{8,12},{9,13},{10,... | collective-permute-start | bytes 860168 | tf_op jit(solution)/shard_map/ppermute | solution.py:216
  22.0 4.2 %collective-permute-done.4.refs_4_ = bf16[112,1280]{1,0:T(8,128)(2,1)S(1)} collective-permute-done((bf16[112,1280]{1,0:T(8,128)(2,1)S(1)}, bf16[112,1280]{1,0:T(8,128)(2,1)S(1)}, u32[]{:S(2)}, u32[]{:S(2)}) %collective-permute-start.4) | collective-permute-done | bytes 286752 | tf_op jit(solution)/shard_map/ppermute | solution.py:216
  26.2 5.3 %collective-permute-done.5.refs_5_ = bf16[112,1280]{1,0:T(8,128)(2,1)S(1)} collective-permute-done((bf16[112,1280]{1,0:T(8,128)(2,1)S(1)}, bf16[112,1280]{1,0:T(8,128)(2,1)S(1)}, u32[]{:S(2)}, u32[]{:S(2)}) %collective-permute-start.5) | collective-permute-done | bytes 286752 | tf_op jit(solution)/shard_map/ppermute | solution.py:216
  31.5 1.8 %collective-permute-start.7 = (bf16[112,1280]{1,0:T(8,128)(2,1)S(1)}, bf16[112,1280]{1,0:T(8,128)(2,1)S(1)}, u32[]{:S(2)}, u32[]{:S(2)}) collective-permute-start(bf16[112,1280]{1,0:T(8,128)(2,1)S(1)} %collective-permute-done.1.refs_1_), channel_id=1, source_target_pairs={{0,8},{1,9},{2,10},{3,11},{4,12},{5,13},{6,14},{7,15},{8,0},{9,1},... | collective-permute-start | bytes 860168 | tf_op jit(solution)/shard_map/ppermute | solution.py:216
  33.3 1.5 %collective-permute-start.6 = (bf16[112,1280]{1,0:T(8,128)(2,1)S(1)}, bf16[112,1280]{1,0:T(8,128)(2,1)S(1)}, u32[]{:S(2)}, u32[]{:S(2)}) collective-permute-start(bf16[112,1280]{1,0:T(8,128)(2,1)S(1)} %collective-permute-done.1.refs_1_), channel_id=1, source_target_pairs={{0,4},{1,5},{2,6},{3,7},{4,0},{5,1},{6,2},{7,3},{8,12},{9,13},{10,... | collective-permute-start | bytes 860168 | tf_op jit(solution)/shard_map/ppermute | solution.py:216
  34.8 0.5 collective-permute-start.13
  35.3 0.1 collective-permute-start.11
  35.4 4.1 %collective-permute-done.7.refs_7_ = bf16[112,1280]{1,0:T(8,128)(2,1)S(1)} collective-permute-done((bf16[112,1280]{1,0:T(8,128)(2,1)S(1)}, bf16[112,1280]{1,0:T(8,128)(2,1)S(1)}, u32[]{:S(2)}, u32[]{:S(2)}) %collective-permute-start.7) | collective-permute-done | bytes 286752 | tf_op jit(solution)/shard_map/ppermute | solution.py:216
  39.5 1.2 %collective-permute-done.6.refs_6_ = bf16[112,1280]{1,0:T(8,128)(2,1)S(1)} collective-permute-done((bf16[112,1280]{1,0:T(8,128)(2,1)S(1)}, bf16[112,1280]{1,0:T(8,128)(2,1)S(1)}, u32[]{:S(2)}, u32[]{:S(2)}) %collective-permute-start.6) | collective-permute-done | bytes 286752 | tf_op jit(solution)/shard_map/ppermute | solution.py:216
  40.7 0.5 collective-permute-start.14
  41.3 5.9 %near.1 = (bf16[384,1792]{1,0:T(8,128)(2,1)S(1)}, f32[384,1024]{1,0:T(8,128)S(1)}, f32[384,256]{1,0:T(8,128)S(1)}, bf16[384,256]{1,0:T(8,128)(2,1)S(1)}, bf16[38...) custom-call(s32[2,256]{1,0:T(2,128)S(1)} %bitcast.4, s32[1,256]{1,0:T(1,128)S(1)} %bitcast.5, ...), custom_call_target="tpu_custom_call" | custom-call | flops 7046430720 | bytes 12582912 | tf_op jit(solution)/shard_map/near/pallas_call | solution.py:127
  47.2 2.9 %losses.1 = f32[32,1,256]{2,1,0:T(1,128)S(1)} custom-call(bf16[384,1792]{1,0:T(8,128)(2,1)S(1)} %get-tuple-element.15.x_ref, f32[384,1024]{1,0:T(8,128)S(1)} %get-tuple-element.16.base_ref, f32[384,256]{1,0:T(8,128)S(1)} %get-tuple-element.17.sc_ref, bf16[384,1024]{1,0:T(8,128)(2,1)S(1)} %get-tuple-element.18.right_ref, ...), custom_call_target="tpu_custom_call" | custom-call | tf_op jit(solution)/shard_map/losses/pallas_call | solution.py:169
  50.1 12.0 %all_to_all.5.parts_ref = f32[32,1,256]{2,1,0:T(1,128)S(1)} all-to-all(f32[32,1,256]{2,1,0:T(1,128)S(1)} %losses.1), channel_id=1, replica_groups=mesh['grp'=16,'fsdp'=2] {'grp','fsdp'}, dimensions={0} | all-to-all | bytes 65536 | tf_op jit(solution)/shard_map/all_to_all | solution.py:278
  62.1 4.1 %update.1 = (f32[1792,1024]{1,0:T(8,128)}, f32[1,256]{1,0:T(1,128)}) custom-call(f32[32,1,256]{2,1,0:T(1,128)S(1)} %all_to_all.5.parts_ref, s32[1,256]{1,0:T(1,128)S(1)} %bitcast.6, bf16[1792,256]{1,0:T(8,128)(2,1)S(1)} %get-tuple-element.24.columns_ref, bf16[256,1024]{1,0:T(8,128)(2,1)S(1)} %get-tuple-element.25.chosen_ref), custom_call_target="tpu_custom_call" | custom-call | tf_op jit(solution)/shard_map/update/pallas_call | solution.py:204
  (19 shorter events, 0.0 us)
Async XLA Ops:
  0.6 0.7 %copy-start = (s32[256,2]{0,1:T(2,128)S(1)}, s32[256,2]{0,1:T(2,128)}, u32[]{:S(2)}) copy-start(s32[256,2]{0,1:T(2,128)} %param.13) | copy-start | bytes 6148
  1.3 39.9 %copy-start.1 = (s32[256,2]{0,1:T(2,128)S(1)}, s32[256,2]{0,1:T(2,128)}, u32[]{:S(2)}) copy-start(s32[256,2]{0,1:T(2,128)} %param.13) | copy-start | bytes 6148
  1.3 39.9 %copy-start.2 = (s32[256]{0:T(256)S(1)}, s32[256]{0:T(256)}, u32[]{:S(2)}) copy-start(s32[256]{0:T(256)} %param.12) | copy-start | bytes 3076
  3.2 10.7 %collective-permute-start = (bf16[112,1280]{1,0:T(8,128)(2,1)S(1)}, bf16[112,1280]{1,0:T(8,128)(2,1)S(1)}, u32[]{:S(2)}, u32[]{:S(2)}) collective-permute-start(bf16[112,1280]{1,0:T(8,128)(2,1)S(1)} %get-tuple-element.20), channel_id=1, source_target_pairs={{0,1},{1,0},{2,3},{3,2},{4,5},{5,4},{6,7},{7,6},{8,9},{9,8},{10,11... | collective-permute-start | bytes 860168 | tf_op jit(solution)/shard_map/ppermute | solution.py:216
  6.2 13.8 %collective-permute-start.1 = (bf16[112,1280]{1,0:T(8,128)(2,1)S(1)}, bf16[112,1280]{1,0:T(8,128)(2,1)S(1)}, u32[]{:S(2)}, u32[]{:S(2)}) collective-permute-start(bf16[112,1280]{1,0:T(8,128)(2,1)S(1)} %get-tuple-element.21), channel_id=1, source_target_pairs={{0,1},{1,0},{2,3},{3,2},{4,5},{5,4},{6,7},{7,6},{8,9},{9,8},{10,11... | collective-permute-start | bytes 860168 | tf_op jit(solution)/shard_map/ppermute | solution.py:216
  6.3 19.9 %collective-permute-start.4 = (bf16[112,1280]{1,0:T(8,128)(2,1)S(1)}, bf16[112,1280]{1,0:T(8,128)(2,1)S(1)}, u32[]{:S(2)}, u32[]{:S(2)}) collective-permute-start(bf16[112,1280]{1,0:T(8,128)(2,1)S(1)} %get-tuple-element.22), channel_id=1, source_target_pairs={{0,1},{1,0},{2,3},{3,2},{4,5},{5,4},{6,7},{7,6},{8,9},{9,8},{10,11... | collective-permute-start | bytes 860168 | tf_op jit(solution)/shard_map/ppermute | solution.py:216
  8.3 23.2 %collective-permute-start.5 = (bf16[112,1280]{1,0:T(8,128)(2,1)S(1)}, bf16[112,1280]{1,0:T(8,128)(2,1)S(1)}, u32[]{:S(2)}, u32[]{:S(2)}) collective-permute-start(bf16[112,1280]{1,0:T(8,128)(2,1)S(1)} %get-tuple-element.23), channel_id=1, source_target_pairs={{0,1},{1,0},{2,3},{3,2},{4,5},{5,4},{6,7},{7,6},{8,9},{9,8},{10,11... | collective-permute-start | bytes 860168 | tf_op jit(solution)/shard_map/ppermute | solution.py:216
  13.9 19.4 %collective-permute-start.8 = (bf16[112,1280]{1,0:T(8,128)(2,1)S(1)}, bf16[112,1280]{1,0:T(8,128)(2,1)S(1)}, u32[]{:S(2)}, u32[]{:S(2)}) collective-permute-start(bf16[112,1280]{1,0:T(8,128)(2,1)S(1)} %collective-permute-done.refs_0_), channel_id=1, source_target_pairs={{0,2},{1,3},{2,0},{3,1},{4,6},{5,7},{6,4},{7,5},{8,10},{9,11},{10,... | collective-permute-start | bytes 860168 | tf_op jit(solution)/shard_map/ppermute | solution.py:216
  13.9 20.9 %collective-permute-start.3 = (bf16[112,1280]{1,0:T(8,128)(2,1)S(1)}, bf16[112,1280]{1,0:T(8,128)(2,1)S(1)}, u32[]{:S(2)}, u32[]{:S(2)}) collective-permute-start(bf16[112,1280]{1,0:T(8,128)(2,1)S(1)} %collective-permute-done.refs_0_), channel_id=1, source_target_pairs={{0,8},{1,9},{2,10},{3,11},{4,12},{5,13},{6,14},{7,15},{8,0},{9,1},... | collective-permute-start | bytes 860168 | tf_op jit(solution)/shard_map/ppermute | solution.py:216
  20.1 14.7 %collective-permute-start.2 = (bf16[112,1280]{1,0:T(8,128)(2,1)S(1)}, bf16[112,1280]{1,0:T(8,128)(2,1)S(1)}, u32[]{:S(2)}, u32[]{:S(2)}) collective-permute-start(bf16[112,1280]{1,0:T(8,128)(2,1)S(1)} %collective-permute-done.refs_0_), channel_id=1, source_target_pairs={{0,4},{1,5},{2,6},{3,7},{4,0},{5,1},{6,2},{7,3},{8,12},{9,13},{10,... | collective-permute-start | bytes 860168 | tf_op jit(solution)/shard_map/ppermute | solution.py:216
  26.2 9.1 %collective-permute-start.9 = (bf16[112,1280]{1,0:T(8,128)(2,1)S(1)}, bf16[112,1280]{1,0:T(8,128)(2,1)S(1)}, u32[]{:S(2)}, u32[]{:S(2)}) collective-permute-start(bf16[112,1280]{1,0:T(8,128)(2,1)S(1)} %collective-permute-done.1.refs_1_), channel_id=1, source_target_pairs={{0,2},{1,3},{2,0},{3,1},{4,6},{5,7},{6,4},{7,5},{8,10},{9,11},{10,... | collective-permute-start | bytes 860168 | tf_op jit(solution)/shard_map/ppermute | solution.py:216
  31.5 8.0 %collective-permute-start.7 = (bf16[112,1280]{1,0:T(8,128)(2,1)S(1)}, bf16[112,1280]{1,0:T(8,128)(2,1)S(1)}, u32[]{:S(2)}, u32[]{:S(2)}) collective-permute-start(bf16[112,1280]{1,0:T(8,128)(2,1)S(1)} %collective-permute-done.1.refs_1_), channel_id=1, source_target_pairs={{0,8},{1,9},{2,10},{3,11},{4,12},{5,13},{6,14},{7,15},{8,0},{9,1},... | collective-permute-start | bytes 860168 | tf_op jit(solution)/shard_map/ppermute | solution.py:216
  33.3 7.4 %collective-permute-start.6 = (bf16[112,1280]{1,0:T(8,128)(2,1)S(1)}, bf16[112,1280]{1,0:T(8,128)(2,1)S(1)}, u32[]{:S(2)}, u32[]{:S(2)}) collective-permute-start(bf16[112,1280]{1,0:T(8,128)(2,1)S(1)} %collective-permute-done.1.refs_1_), channel_id=1, source_target_pairs={{0,4},{1,5},{2,6},{3,7},{4,0},{5,1},{6,2},{7,3},{8,12},{9,13},{10,... | collective-permute-start | bytes 860168 | tf_op jit(solution)/shard_map/ppermute | solution.py:216
  34.8 6.0 %collective-permute-start.12 = (bf16[112,1280]{1,0:T(8,128)(2,1)S(1)}, bf16[112,1280]{1,0:T(8,128)(2,1)S(1)}, u32[]{:S(2)}, u32[]{:S(2)}) collective-permute-start(bf16[112,1280]{1,0:T(8,128)(2,1)S(1)} %collective-permute-done.4.refs_4_), channel_id=1, source_target_pairs={{0,2},{1,3},{2,0},{3,1},{4,6},{5,7},{6,4},{7,5},{8,10},{9,11},{10,... | collective-permute-start | bytes 860168 | tf_op jit(solution)/shard_map/ppermute | solution.py:216
  34.8 12.4 %collective-permute-start.13 = (bf16[112,1280]{1,0:T(8,128)(2,1)S(1)}, bf16[112,1280]{1,0:T(8,128)(2,1)S(1)}, u32[]{:S(2)}, u32[]{:S(2)}) collective-permute-start(bf16[112,1280]{1,0:T(8,128)(2,1)S(1)} %collective-permute-done.5.refs_5_), channel_id=1, source_target_pairs={{0,2},{1,3},{2,0},{3,1},{4,6},{5,7},{6,4},{7,5},{8,10},{9,11},{10,... | collective-permute-start | bytes 860168 | tf_op jit(solution)/shard_map/ppermute | solution.py:216
  35.3 11.9 %collective-permute-start.11 = (bf16[112,1280]{1,0:T(8,128)(2,1)S(1)}, bf16[112,1280]{1,0:T(8,128)(2,1)S(1)}, u32[]{:S(2)}, u32[]{:S(2)}) collective-permute-start(bf16[112,1280]{1,0:T(8,128)(2,1)S(1)} %collective-permute-done.3.refs_3_), channel_id=1, source_target_pairs={{0,2},{1,3},{2,0},{3,1},{4,6},{5,7},{6,4},{7,5},{8,10},{9,11},{10,... | collective-permute-start | bytes 860168 | tf_op jit(solution)/shard_map/ppermute | solution.py:216
  39.5 7.7 %collective-permute-start.10 = (bf16[112,1280]{1,0:T(8,128)(2,1)S(1)}, bf16[112,1280]{1,0:T(8,128)(2,1)S(1)}, u32[]{:S(2)}, u32[]{:S(2)}) collective-permute-start(bf16[112,1280]{1,0:T(8,128)(2,1)S(1)} %collective-permute-done.2.refs_2_), channel_id=1, source_target_pairs={{0,2},{1,3},{2,0},{3,1},{4,6},{5,7},{6,4},{7,5},{8,10},{9,11},{10,... | collective-permute-start | bytes 860168 | tf_op jit(solution)/shard_map/ppermute | solution.py:216
  40.7 6.5 %collective-permute-start.15 = (bf16[112,1280]{1,0:T(8,128)(2,1)S(1)}, bf16[112,1280]{1,0:T(8,128)(2,1)S(1)}, u32[]{:S(2)}, u32[]{:S(2)}) collective-permute-start(bf16[112,1280]{1,0:T(8,128)(2,1)S(1)} %collective-permute-done.7.refs_7_), channel_id=1, source_target_pairs={{0,2},{1,3},{2,0},{3,1},{4,6},{5,7},{6,4},{7,5},{8,10},{9,11},{10,... | collective-permute-start | bytes 860168 | tf_op jit(solution)/shard_map/ppermute | solution.py:216
  40.7 6.5 %collective-permute-start.14 = (bf16[112,1280]{1,0:T(8,128)(2,1)S(1)}, bf16[112,1280]{1,0:T(8,128)(2,1)S(1)}, u32[]{:S(2)}, u32[]{:S(2)}) collective-permute-start(bf16[112,1280]{1,0:T(8,128)(2,1)S(1)} %collective-permute-done.6.refs_6_), channel_id=1, source_target_pairs={{0,2},{1,3},{2,0},{3,1},{4,6},{5,7},{6,4},{7,5},{8,10},{9,11},{10,... | collective-permute-start | bytes 860168 | tf_op jit(solution)/shard_map/ppermute | solution.py:216

commit v2 on v1

--- a/solution.py
+++ b/solution.py
@@ -12,6 +12,7 @@
 f32 = jnp.float32
 bf16 = jnp.bfloat16
 PIECES = 8
+SKEW = 0
 
 
 def turned(row, height):
@@ -24,20 +25,24 @@
 
 
 def pack_kernel(order, index_ref, weight_ref, factor_ref, *refs):
-    outs, factors, w_sem, a_sem = refs[:-3], refs[-3], refs[-2], refs[-1]
-    height, width = outs[0].shape[0], weight_ref.shape[1]
+    outs, factors, index, w_sem, a_sem, i_sem = refs[:-5], *refs[-5:]
+    width = weight_ref.shape[1]
+    first = pltpu.make_async_copy(index_ref, index, i_sem)
+    first.start()
     copies = []
-    for k, (out, block) in enumerate(zip(outs, order())):
-        rows = pl.ds(pl.multiple_of(block * height, 16), height)
-        a = pltpu.make_async_copy(factor_ref.at[rows], factors.at[k], a_sem.at[k])
+    for k, (out, start) in enumerate(zip(outs, order())):
+        height = out.shape[0]
+        rows = pl.ds(pl.multiple_of(start, 16), height)
+        a = pltpu.make_async_copy(factor_ref.at[rows], factors.at[k, pl.ds(0, height)], a_sem.at[k])
         w = pltpu.make_async_copy(weight_ref.at[rows], out.at[:, pl.ds(0, width)], w_sem.at[k])
         a.start()
         w.start()
         copies.append((a, w))
-    selector = matches(index_ref[0:1, :], factor_ref.shape[1])
+    first.wait()
+    selector = matches(index[0:1, :], factor_ref.shape[1])
     for k, (out, (a, w)) in enumerate(zip(outs, copies)):
         a.wait()
-        out[:, width:] = jnp.dot(factors[k], selector, preferred_element_type=f32).astype(bf16)
+        out[:, width:] = jnp.dot(factors[k, : out.shape[0]], selector, preferred_element_type=f32).astype(bf16)
     for _, w in copies:
         w.wait()
 
@@ -58,21 +63,24 @@
     return pltpu.CompilerParams(vmem_limit_bytes=mib << 20)
 
 
-def pack(order, count, index, weight, factor_a, height):
+def pack(order, heights, index, weight, factor_a):
+    count = len(heights)
     width, pool, cands = weight.shape[1], factor_a.shape[1], index.shape[1]
     return pl.pallas_call(
         functools.partial(pack_kernel, order),
-        in_specs=[vmem(), hbm(), hbm()],
+        in_specs=[hbm()] * 3,
         out_specs=[vmem()] * count,
-        out_shape=[jax.ShapeDtypeStruct((height, width + cands), bf16)] * count,
+        out_shape=[jax.ShapeDtypeStruct((h, width + cands), bf16) for h in heights],
         scratch_shapes=[
-            pltpu.VMEM((count, height, pool), bf16),
+            pltpu.VMEM((count, max(heights), pool), bf16),
+            pltpu.VMEM(index.shape, jnp.int32),
             pltpu.SemaphoreType.DMA((count,)),
             pltpu.SemaphoreType.DMA((count,)),
+            pltpu.SemaphoreType.DMA,
         ],
         compiler_params=params(8),
         name="pack",
-    )(index, *in_hbm(weight, factor_a))
+    )(*in_hbm(index, weight, factor_a))
 
 
 def near_kernel(
@@ -144,17 +152,51 @@
     )(index, counts, *in_hbm(tokens, weight, factor_a, factor_b, target))
 
 
+def stack(pieces, blocks, held):
+    height = pieces[0].shape[0]
+    for piece, block in zip(pieces, blocks):
+        held[pl.ds(pl.multiple_of(block * height, 16), height), :] = piece[...]
+
+
+def middle_kernel(order, x_ref, base_ref, sc_ref, *refs):
+    pieces, base_out, sc_out, held = refs[:-3], *refs[-3:]
+    stack(pieces, order(), held)
+    rows, width = base_ref.shape
+    half = held.shape[0]
+    step = 128
+    for r in range(0, rows, step):
+        s = slice(r, r + step)
+        acc = jnp.dot(x_ref[s, :half], held[...], preferred_element_type=f32)
+        base_out[s, :] = base_ref[s, :] + acc[:, :width]
+        sc_out[s, :] = sc_ref[s, :] + acc[:, width:]
+
+
+def middle(order, x, base, sc, pieces):
+    depth, columns = x.shape[1], base.shape[1] + sc.shape[1]
+    return pl.pallas_call(
+        functools.partial(middle_kernel, order),
+        in_specs=[vmem()] * (3 + len(pieces)),
+        out_specs=[vmem()] * 2,
+        out_shape=[jax.ShapeDtypeStruct(base.shape, f32), jax.ShapeDtypeStruct(sc.shape, f32)],
+        scratch_shapes=[pltpu.VMEM((sum(p.shape[0] for p in pieces), columns), bf16)],
+        compiler_params=params(20),
+        cost_estimate=pl.CostEstimate(
+            flops=4 * x.shape[0] * depth * columns, bytes_accessed=4 << 20, transcendentals=0
+        ),
+        name="middle",
+    )(x, base, sc, *pieces)
+
+
 def loss_kernel(noise, order, x_ref, base_ref, sc_ref, right_ref, hot_ref, *refs):
     pieces, out_ref, held = refs[:-2], refs[-2], refs[-1]
-    height = pieces[0].shape[0]
-    for piece, block in zip(pieces, order()):
-        held[pl.ds(pl.multiple_of(block * height, 16), height), :] = piece[...]
+    stack(pieces, order(), held)
     rows, width = base_ref.shape
+    half = held.shape[0]
     total = None
     step = 128
     for r in range(0, rows, step):
         s = slice(r, r + step)
-        acc = jnp.dot(x_ref[s, :], held[...], preferred_element_type=f32)
+        acc = jnp.dot(x_ref[s, x_ref.shape[1] - half :], held[...], preferred_element_type=f32)
         hot = hot_ref[s, :].astype(f32)
         picked = jnp.sum(hot * (acc[:, width:] + sc_ref[s, :]), axis=1, keepdims=True) * noise
         diff = acc[:, :width] + base_ref[s, :] + picked * right_ref[s, :].astype(f32)
@@ -165,13 +207,13 @@
 
 
 def losses(noise, order, x, base, sc, right, hot, pieces, devices):
-    depth, width, cands = x.shape[1], base.shape[1], hot.shape[1]
+    width, cands = base.shape[1], hot.shape[1]
     return pl.pallas_call(
         functools.partial(loss_kernel, noise, order),
         in_specs=[vmem()] * (5 + len(pieces)),
         out_specs=vmem(),
         out_shape=jax.ShapeDtypeStruct((devices, 1, cands), f32),
-        scratch_shapes=[pltpu.VMEM((depth, width + cands), bf16)],
+        scratch_shapes=[pltpu.VMEM((sum(p.shape[0] for p in pieces), width + cands), bf16)],
         compiler_params=params(20),
         name="losses",
     )(x, base, sc, right, hot, *pieces)
@@ -221,15 +263,17 @@
     return jnp.bitwise_and(grp, 1), jnp.bitwise_and(jnp.right_shift(grp, 1), 3)
 
 
-def sent():
+def sent(heights, first, last):
     core, spot = place()
-    return [2 * i + core for i in (spot, spot + 4, 3 - spot, 7 - spot)]
+    early, late = heights
+    near, far = 2 * spot + core, 2 * (3 - spot) + core
+    base = PIECES * early
+    return [near * early, base + near * late, far * early, base + far * late][first:last]
 
 
 def arrived():
     core, spot = place()
-    x, z = jnp.bitwise_xor(spot, 1), jnp.bitwise_xor(spot, 2)
-    ids = [spot, spot + 4, x, z, 3 - spot, 7 - spot, x + 4, z + 4]
+    ids = [spot, jnp.bitwise_xor(spot, 1), jnp.bitwise_xor(spot, 2), 3 - spot]
     return [2 * i + core for i in ids] + [2 * i + 1 - core for i in ids]
 
 
@@ -244,19 +288,26 @@
     cands = counts.shape[0]
     noise = 0.5 * full ** (-0.5)
     index = cand_index.T
-    if parts == 2 and groups % 8 == 0 and depth % (2 * PIECES * 16) == 0:
-        height = depth // (2 * PIECES)
-        first, second, third, fourth = pack(sent, 4, index, weight, factor_a, height)
+    if parts == 2 and groups % 8 == 0 and depth % (2 * PIECES * 16) == 0 and depth > 32 * PIECES:
+        late = (depth // PIECES - SKEW) // 2
+        heights = (depth // PIECES - late, late)
+        (first,) = pack(functools.partial(sent, heights, 0, 1), heights[:1], index, weight, factor_a)
+        second, third, fourth = pack(
+            functools.partial(sent, heights, 1, 4), heights[::-1] + heights[1:], index, weight, factor_a
+        )
         y1, y2 = hop(first, 1, devices), hop(second, 1, devices)
         y3, y4 = hop(third, 1, devices), hop(fourth, 1, devices)
         x1, z1 = hop(y1, 4, devices), hop(y1, 8, devices)
         x2, z2 = hop(y2, 4, devices), hop(y2, 8, devices)
-        own = [y1, y2, x1, z1, y3, y4, x2, z2]
-        swapped = [hop(v, 2, devices) for v in own]
+        early, late = {"y1": y1, "x1": x1, "z1": z1, "y3": y3}, {"y2": y2, "x2": x2, "z2": z2, "y4": y4}
+        early, late = (
+            [*some.values()] + [hop(v, 2, devices) for v in some.values()] for some in (early, late)
+        )
         far, base, sc, hot, right_rows, columns, chosen = near_half(
             index, counts[None, :], tokens, weight, factor_a, factor_b, target
         )
-        sums = losses(noise, arrived, far, base, sc, right_rows, hot, own + swapped, devices)
+        base, sc = middle(arrived, far, base, sc, early)
+        sums = losses(noise, arrived, far, base, sc, right_rows, hot, late, devices)
     else:
         left, right = cand_index[:, 0], cand_index[:, 1]
         cand_ids = jnp.arange(cands, dtype=jnp.int32)

time: 66.3 us -> 59.8 us (0.902)
  waiting for transfers between devices: 24.5 us -> 18.3 us
  Pallas kernels: 14.7 us -> 15.8 us
  blocking collectives: 12 us -> 11.1 us
  local copies, waits for them, and re-layouts: 0.68 us -> 0.01 us
    ppermute x16, waiting for transfers between devices: 24.5 us -> 18.3 us  [hop(): return lax.ppermute(value, AXES, [(i, i ^ bit) for i in range(devices)])]
    pallas_call x1 -> x3, Pallas kernels: 1.84 us -> 4.1 us  [the longest x2 2.67 us: pack(): pl.pallas_call(functools.partial(pack_kernel, order), in_specs=[hbm()] *...]
    pallas_call x1, Pallas kernels: 2.87 us -> 1.78 us  [losses(): pl.pallas_call(functools.partial(loss_kernel, noise, order), in_specs=[vm...]
    all_to_all x1, blocking collectives: 12 us -> 11.1 us  [compute(): spread = lax.all_to_all(sums, AXES, split_axis=0, concat_axis=0, tiled=True)]
    unnamed x6 -> x4, local copies, waits for them, and re-layouts: 0.68 us -> 0.01 us
  transfers between devices with their start and end apart: 16 -> 16, of which waited for: 6 -> 5; matrix products, arithmetic and copies ran while one was open for 0% -> 0% of each run, Pallas kernels for 9% -> 15%
where the time goes in v2:
time: 59.8 us; the launch traced here: 59.6 us
  waiting for transfers between devices  18.3 us (31%)
  Pallas kernels  15.8 us (26%)
  starting transfers between devices  13.7 us (23%)
  blocking collectives  11.1 us (19%)
  between operations  0.73 us (1%)
    ppermute x16, waiting for transfers between devices, hop(): return lax.ppermute(value, AXES, [(i, i ^ bit) for i in range(devices)])  18.3 us
    ppermute x16, starting transfers between devices, hop(): return lax.ppermute(value, AXES, [(i, i ^ bit) for i in range(devices)])  13.7 us
    all_to_all x1, blocking collectives, compute(): spread = lax.all_to_all(sums, AXES, split_axis=0, concat_axis=0, tiled=True)  11.1 us
    pallas_call x1, Pallas kernels, near_half(): pl.pallas_call(near_kernel, in_specs=[vmem(), vmem()] + [hbm()] * 5, out_...  5.89 us
    pallas_call x1, Pallas kernels, update_of(): pl.pallas_call(functools.partial(update_kernel, step), in_specs=[vmem()]...  4.06 us
    pallas_call x2, Pallas kernels, pack(): pl.pallas_call(functools.partial(pack_kernel, order), in_specs=[hbm()] *...  2.67 us
    pallas_call x1, Pallas kernels, losses(): pl.pallas_call(functools.partial(loss_kernel, noise, order), in_specs=[vm...  1.78 us
    pallas_call x1, Pallas kernels, middle(): pl.pallas_call(functools.partial(middle_kernel, order), in_specs=[vmem()]...  1.42 us
  transfers between devices with their start and end apart: 16, of which 5 were waited for; matrix products, arithmetic and copies ran while one was open for 0% of the time, Pallas kernels for 15%

profile of v2, /device:TPU:0, one launch (start us, length us, event | category | flops | bytes accessed | tf_op | source)
XLA Modules:
  0.0 59.6 jit_solution(16730510207598682751)
XLA Ops:
  0.6 1.1 %pack.2 = bf16[112,1280]{1,0:T(8,128)(2,1)S(1)} custom-call(s32[2,256]{1,0:T(2,128)} %bitcast.3, bf16[1792,1024]{1,0:T(8,128)(2,1)} %weight_ref.5, bf16[1792,512]{1,0:T(8,128)(2,1)} %factor_ref.5), custom_call_target="tpu_custom_call" | custom-call | tf_op jit(solution)/shard_map/pack/pallas_call | solution.py:69
  1.8 3.1 %collective-permute-start = (bf16[112,1280]{1,0:T(8,128)(2,1)S(1)}, bf16[112,1280]{1,0:T(8,128)(2,1)S(1)}, u32[]{:S(2)}, u32[]{:S(2)}) collective-permute-start(bf16[112,1280]{1,0:T(8,128)(2,1)S(1)} %pack.2), channel_id=1, source_target_pairs={{0,1},{1,0},{2,3},{3,2},{4,5},{5,4},{6,7},{7,6},{8,9},{9,8},{10,11... | collective-permute-start | bytes 860168 | tf_op jit(solution)/shard_map/ppermute | solution.py:258
  4.8 1.6 %pack.3 = (bf16[112,1280]{1,0:T(8,128)(2,1)S(1)}, bf16[112,1280]{1,0:T(8,128)(2,1)S(1)}, bf16[112,1280]{1,0:T(8,128)(2,1)S(1)}) custom-call(s32[2,256]{1,0:T(2,128)} %bitcast.4, bf16[1792,1024]{1,0:T(8,128)(2,1)} %weight_ref.5, bf16[1792,512]{1,0:T(8,128)(2,1)} %factor_ref.5), custom_call_target="tpu_custom_call" | custom-call | tf_op jit(solution)/shard_map/pack/pallas_call | solution.py:69
  6.4 0.1 collective-permute-start.3
  6.5 2.0 %collective-permute-start.8 = (bf16[112,1280]{1,0:T(8,128)(2,1)S(1)}, bf16[112,1280]{1,0:T(8,128)(2,1)S(1)}, u32[]{:S(2)}, u32[]{:S(2)}) collective-permute-start(bf16[112,1280]{1,0:T(8,128)(2,1)S(1)} %get-tuple-element.24), channel_id=1, source_target_pairs={{0,1},{1,0},{2,3},{3,2},{4,5},{5,4},{6,7},{7,6},{8,9},{9,8},{10,11... | collective-permute-start | bytes 860168 | tf_op jit(solution)/shard_map/ppermute | solution.py:258
  8.6 3.9 %collective-permute-done.refs_0_ = bf16[112,1280]{1,0:T(8,128)(2,1)S(1)} collective-permute-done((bf16[112,1280]{1,0:T(8,128)(2,1)S(1)}, bf16[112,1280]{1,0:T(8,128)(2,1)S(1)}, u32[]{:S(2)}, u32[]{:S(2)}) %collective-permute-start) | collective-permute-done | bytes 286752 | tf_op jit(solution)/shard_map/ppermute | solution.py:258
  12.5 2.0 %collective-permute-start.1 = (bf16[112,1280]{1,0:T(8,128)(2,1)S(1)}, bf16[112,1280]{1,0:T(8,128)(2,1)S(1)}, u32[]{:S(2)}, u32[]{:S(2)}) collective-permute-start(bf16[112,1280]{1,0:T(8,128)(2,1)S(1)} %collective-permute-done.refs_0_), channel_id=1, source_target_pairs={{0,4},{1,5},{2,6},{3,7},{4,0},{5,1},{6,2},{7,3},{8,12},{9,13},{10,... | collective-permute-start | bytes 860168 | tf_op jit(solution)/shard_map/ppermute | solution.py:258
  14.5 1.6 %collective-permute-start.2 = (bf16[112,1280]{1,0:T(8,128)(2,1)S(1)}, bf16[112,1280]{1,0:T(8,128)(2,1)S(1)}, u32[]{:S(2)}, u32[]{:S(2)}) collective-permute-start(bf16[112,1280]{1,0:T(8,128)(2,1)S(1)} %collective-permute-done.refs_0_), channel_id=1, source_target_pairs={{0,8},{1,9},{2,10},{3,11},{4,12},{5,13},{6,14},{7,15},{8,0},{9,1},... | collective-permute-start | bytes 860168 | tf_op jit(solution)/shard_map/ppermute | solution.py:258
  16.1 2.6 %collective-permute-done.3.refs_3_ = bf16[112,1280]{1,0:T(8,128)(2,1)S(1)} collective-permute-done((bf16[112,1280]{1,0:T(8,128)(2,1)S(1)}, bf16[112,1280]{1,0:T(8,128)(2,1)S(1)}, u32[]{:S(2)}, u32[]{:S(2)}) %collective-permute-start.3) | collective-permute-done | bytes 286752 | tf_op jit(solution)/shard_map/ppermute | solution.py:258
  18.7 6.1 %collective-permute-done.8.refs_0_ = bf16[112,1280]{1,0:T(8,128)(2,1)S(1)} collective-permute-done((bf16[112,1280]{1,0:T(8,128)(2,1)S(1)}, bf16[112,1280]{1,0:T(8,128)(2,1)S(1)}, u32[]{:S(2)}, u32[]{:S(2)}) %collective-permute-start.8) | collective-permute-done | bytes 286752 | tf_op jit(solution)/shard_map/ppermute | solution.py:258
  24.8 5.3 %collective-permute-done.11.refs_3_ = bf16[112,1280]{1,0:T(8,128)(2,1)S(1)} collective-permute-done((bf16[112,1280]{1,0:T(8,128)(2,1)S(1)}, bf16[112,1280]{1,0:T(8,128)(2,1)S(1)}, u32[]{:S(2)}, u32[]{:S(2)}) %collective-permute-start.11) | collective-permute-done | bytes 286752 | tf_op jit(solution)/shard_map/ppermute | solution.py:258
  30.1 1.7 %collective-permute-start.9 = (bf16[112,1280]{1,0:T(8,128)(2,1)S(1)}, bf16[112,1280]{1,0:T(8,128)(2,1)S(1)}, u32[]{:S(2)}, u32[]{:S(2)}) collective-permute-start(bf16[112,1280]{1,0:T(8,128)(2,1)S(1)} %collective-permute-done.8.refs_0_), channel_id=1, source_target_pairs={{0,4},{1,5},{2,6},{3,7},{4,0},{5,1},{6,2},{7,3},{8,12},{9,13},{10,... | collective-permute-start | bytes 860168 | tf_op jit(solution)/shard_map/ppermute | solution.py:258
  31.8 1.6 %collective-permute-start.10 = (bf16[112,1280]{1,0:T(8,128)(2,1)S(1)}, bf16[112,1280]{1,0:T(8,128)(2,1)S(1)}, u32[]{:S(2)}, u32[]{:S(2)}) collective-permute-start(bf16[112,1280]{1,0:T(8,128)(2,1)S(1)} %collective-permute-done.8.refs_0_), channel_id=1, source_target_pairs={{0,8},{1,9},{2,10},{3,11},{4,12},{5,13},{6,14},{7,15},{8,0},{9,1},... | collective-permute-start | bytes 860168 | tf_op jit(solution)/shard_map/ppermute | solution.py:258
  33.4 0.5 collective-permute-start.6
  33.9 5.9 %near.1 = (bf16[384,1792]{1,0:T(8,128)(2,1)S(1)}, f32[384,1024]{1,0:T(8,128)S(1)}, f32[384,256]{1,0:T(8,128)S(1)}, bf16[384,256]{1,0:T(8,128)(2,1)S(1)}, bf16[38...) custom-call(s32[2,256]{1,0:T(2,128)S(1)} %bitcast.5, s32[1,256]{1,0:T(1,128)S(1)} %bitcast.6, ...), custom_call_target="tpu_custom_call" | custom-call | flops 7046430720 | bytes 12582912 | tf_op jit(solution)/shard_map/near/pallas_call | solution.py:135
  39.8 0.1 collective-permute-start.12
  40.0 0.4 collective-permute-start.15
  40.4 0.1 collective-permute-start.13
  40.5 0.4 collective-permute-start.14
  40.9 1.4 %middle.1 = (f32[384,1024]{1,0:T(8,128)S(1)}, f32[384,256]{1,0:T(8,128)S(1)}) custom-call(bf16[384,1792]{1,0:T(8,128)(2,1)S(1)} %get-tuple-element.16.x_ref, f32[384,1024]{1,0:T(8,128)S(1)} %get-tuple-element.17.base_ref, f32[384,256]{1,0:T(8,128)S(1)} %get-tuple-element.18.sc_ref, bf16[112,1280]{1,0:T(8,128)(2,1)S(1)} %collective-permute-done.refs_0_, ...), custom_call_target="tpu_custom_call" | custom-call | flops 3523215360 | bytes 4194304 | tf_op jit(solution)/shard_map/middle/pallas_call | solution.py:176
  42.4 0.3 collective-permute-done.14.refs_6_
  42.7 1.8 %losses.1 = f32[32,1,256]{2,1,0:T(1,128)S(1)} custom-call(bf16[384,1792]{1,0:T(8,128)(2,1)S(1)} %get-tuple-element.16.x_ref, f32[384,1024]{1,0:T(8,128)S(1)} %get-tuple-element.20.base_ref, f32[384,256]{1,0:T(8,128)S(1)} %get-tuple-element.21.sc_ref, bf16[384,1024]{1,0:T(8,128)(2,1)S(1)} %get-tuple-element.22.right_ref, ...), custom_call_target="tpu_custom_call" | custom-call | tf_op jit(solution)/shard_map/losses/pallas_call | solution.py:211
  44.5 11.1 %all_to_all.5.parts_ref = f32[32,1,256]{2,1,0:T(1,128)S(1)} all-to-all(f32[32,1,256]{2,1,0:T(1,128)S(1)} %losses.1), channel_id=1, replica_groups=mesh['grp'=16,'fsdp'=2] {'grp','fsdp'}, dimensions={0} | all-to-all | bytes 65536 | tf_op jit(solution)/shard_map/all_to_all | solution.py:329
  55.5 4.1 %update.1 = (f32[1792,1024]{1,0:T(8,128)}, f32[1,256]{1,0:T(1,128)}) custom-call(f32[32,1,256]{2,1,0:T(1,128)S(1)} %all_to_all.5.parts_ref, s32[1,256]{1,0:T(1,128)S(1)} %bitcast.7, bf16[1792,256]{1,0:T(8,128)(2,1)S(1)} %get-tuple-element.26.columns_ref, bf16[256,1024]{1,0:T(8,128)(2,1)S(1)} %get-tuple-element.27.chosen_ref), custom_call_target="tpu_custom_call" | custom-call | tf_op jit(solution)/shard_map/update/pallas_call | solution.py:246
  (19 shorter events, 0.1 us)
Async XLA Ops:
  1.7 32.2 %copy-start = (s32[256,2]{0,1:T(2,128)S(1)}, s32[256,2]{0,1:T(2,128)}, u32[]{:S(2)}) copy-start(s32[256,2]{0,1:T(2,128)} %param.13) | copy-start | bytes 6148
  1.8 32.2 %copy-start.1 = (s32[256]{0:T(256)S(1)}, s32[256]{0:T(256)}, u32[]{:S(2)}) copy-start(s32[256]{0:T(256)} %param.12) | copy-start | bytes 3076
  1.8 10.7 %collective-permute-start = (bf16[112,1280]{1,0:T(8,128)(2,1)S(1)}, bf16[112,1280]{1,0:T(8,128)(2,1)S(1)}, u32[]{:S(2)}, u32[]{:S(2)}) collective-permute-start(bf16[112,1280]{1,0:T(8,128)(2,1)S(1)} %pack.2), channel_id=1, source_target_pairs={{0,1},{1,0},{2,3},{3,2},{4,5},{5,4},{6,7},{7,6},{8,9},{9,8},{10,11... | collective-permute-start | bytes 860168 | tf_op jit(solution)/shard_map/ppermute | solution.py:258
  6.4 12.3 %collective-permute-start.3 = (bf16[112,1280]{1,0:T(8,128)(2,1)S(1)}, bf16[112,1280]{1,0:T(8,128)(2,1)S(1)}, u32[]{:S(2)}, u32[]{:S(2)}) collective-permute-start(bf16[112,1280]{1,0:T(8,128)(2,1)S(1)} %get-tuple-element.19), channel_id=1, source_target_pairs={{0,1},{1,0},{2,3},{3,2},{4,5},{5,4},{6,7},{7,6},{8,9},{9,8},{10,11... | collective-permute-start | bytes 860168 | tf_op jit(solution)/shard_map/ppermute | solution.py:258
  6.5 18.3 %collective-permute-start.8 = (bf16[112,1280]{1,0:T(8,128)(2,1)S(1)}, bf16[112,1280]{1,0:T(8,128)(2,1)S(1)}, u32[]{:S(2)}, u32[]{:S(2)}) collective-permute-start(bf16[112,1280]{1,0:T(8,128)(2,1)S(1)} %get-tuple-element.24), channel_id=1, source_target_pairs={{0,1},{1,0},{2,3},{3,2},{4,5},{5,4},{6,7},{7,6},{8,9},{9,8},{10,11... | collective-permute-start | bytes 860168 | tf_op jit(solution)/shard_map/ppermute | solution.py:258
  8.5 21.6 %collective-permute-start.11 = (bf16[112,1280]{1,0:T(8,128)(2,1)S(1)}, bf16[112,1280]{1,0:T(8,128)(2,1)S(1)}, u32[]{:S(2)}, u32[]{:S(2)}) collective-permute-start(bf16[112,1280]{1,0:T(8,128)(2,1)S(1)} %get-tuple-element.25), channel_id=1, source_target_pairs={{0,1},{1,0},{2,3},{3,2},{4,5},{5,4},{6,7},{7,6},{8,9},{9,8},{10,11... | collective-permute-start | bytes 860168 | tf_op jit(solution)/shard_map/ppermute | solution.py:258
  12.5 19.3 %collective-permute-start.1 = (bf16[112,1280]{1,0:T(8,128)(2,1)S(1)}, bf16[112,1280]{1,0:T(8,128)(2,1)S(1)}, u32[]{:S(2)}, u32[]{:S(2)}) collective-permute-start(bf16[112,1280]{1,0:T(8,128)(2,1)S(1)} %collective-permute-done.refs_0_), channel_id=1, source_target_pairs={{0,4},{1,5},{2,6},{3,7},{4,0},{5,1},{6,2},{7,3},{8,12},{9,13},{10,... | collective-permute-start | bytes 860168 | tf_op jit(solution)/shard_map/ppermute | solution.py:258
  14.5 18.9 %collective-permute-start.2 = (bf16[112,1280]{1,0:T(8,128)(2,1)S(1)}, bf16[112,1280]{1,0:T(8,128)(2,1)S(1)}, u32[]{:S(2)}, u32[]{:S(2)}) collective-permute-start(bf16[112,1280]{1,0:T(8,128)(2,1)S(1)} %collective-permute-done.refs_0_), channel_id=1, source_target_pairs={{0,8},{1,9},{2,10},{3,11},{4,12},{5,13},{6,14},{7,15},{8,0},{9,1},... | collective-permute-start | bytes 860168 | tf_op jit(solution)/shard_map/ppermute | solution.py:258
  18.7 14.7 %collective-permute-start.7 = (bf16[112,1280]{1,0:T(8,128)(2,1)S(1)}, bf16[112,1280]{1,0:T(8,128)(2,1)S(1)}, u32[]{:S(2)}, u32[]{:S(2)}) collective-permute-start(bf16[112,1280]{1,0:T(8,128)(2,1)S(1)} %collective-permute-done.3.refs_3_), channel_id=1, source_target_pairs={{0,2},{1,3},{2,0},{3,1},{4,6},{5,7},{6,4},{7,5},{8,10},{9,11},{10,... | collective-permute-start | bytes 860168 | tf_op jit(solution)/shard_map/ppermute | solution.py:258
  24.8 15.0 %collective-permute-start.4 = (bf16[112,1280]{1,0:T(8,128)(2,1)S(1)}, bf16[112,1280]{1,0:T(8,128)(2,1)S(1)}, u32[]{:S(2)}, u32[]{:S(2)}) collective-permute-start(bf16[112,1280]{1,0:T(8,128)(2,1)S(1)} %collective-permute-done.refs_0_), channel_id=1, source_target_pairs={{0,2},{1,3},{2,0},{3,1},{4,6},{5,7},{6,4},{7,5},{8,10},{9,11},{10,... | collective-permute-start | bytes 860168 | tf_op jit(solution)/shard_map/ppermute | solution.py:258
  30.1 9.9 %collective-permute-start.9 = (bf16[112,1280]{1,0:T(8,128)(2,1)S(1)}, bf16[112,1280]{1,0:T(8,128)(2,1)S(1)}, u32[]{:S(2)}, u32[]{:S(2)}) collective-permute-start(bf16[112,1280]{1,0:T(8,128)(2,1)S(1)} %collective-permute-done.8.refs_0_), channel_id=1, source_target_pairs={{0,4},{1,5},{2,6},{3,7},{4,0},{5,1},{6,2},{7,3},{8,12},{9,13},{10,... | collective-permute-start | bytes 860168 | tf_op jit(solution)/shard_map/ppermute | solution.py:258
  31.8 8.6 %collective-permute-start.10 = (bf16[112,1280]{1,0:T(8,128)(2,1)S(1)}, bf16[112,1280]{1,0:T(8,128)(2,1)S(1)}, u32[]{:S(2)}, u32[]{:S(2)}) collective-permute-start(bf16[112,1280]{1,0:T(8,128)(2,1)S(1)} %collective-permute-done.8.refs_0_), channel_id=1, source_target_pairs={{0,8},{1,9},{2,10},{3,11},{4,12},{5,13},{6,14},{7,15},{8,0},{9,1},... | collective-permute-start | bytes 860168 | tf_op jit(solution)/shard_map/ppermute | solution.py:258
  33.4 7.1 %collective-permute-start.5 = (bf16[112,1280]{1,0:T(8,128)(2,1)S(1)}, bf16[112,1280]{1,0:T(8,128)(2,1)S(1)}, u32[]{:S(2)}, u32[]{:S(2)}) collective-permute-start(bf16[112,1280]{1,0:T(8,128)(2,1)S(1)} %collective-permute-done.1.refs_1_), channel_id=1, source_target_pairs={{0,2},{1,3},{2,0},{3,1},{4,6},{5,7},{6,4},{7,5},{8,10},{9,11},{10,... | collective-permute-start | bytes 860168 | tf_op jit(solution)/shard_map/ppermute | solution.py:258
  33.4 7.5 %collective-permute-start.6 = (bf16[112,1280]{1,0:T(8,128)(2,1)S(1)}, bf16[112,1280]{1,0:T(8,128)(2,1)S(1)}, u32[]{:S(2)}, u32[]{:S(2)}) collective-permute-start(bf16[112,1280]{1,0:T(8,128)(2,1)S(1)} %collective-permute-done.2.refs_2_), channel_id=1, source_target_pairs={{0,2},{1,3},{2,0},{3,1},{4,6},{5,7},{6,4},{7,5},{8,10},{9,11},{10,... | collective-permute-start | bytes 860168 | tf_op jit(solution)/shard_map/ppermute | solution.py:258
  39.8 2.5 %collective-permute-start.12 = (bf16[112,1280]{1,0:T(8,128)(2,1)S(1)}, bf16[112,1280]{1,0:T(8,128)(2,1)S(1)}, u32[]{:S(2)}, u32[]{:S(2)}) collective-permute-start(bf16[112,1280]{1,0:T(8,128)(2,1)S(1)} %collective-permute-done.8.refs_0_), channel_id=1, source_target_pairs={{0,2},{1,3},{2,0},{3,1},{4,6},{5,7},{6,4},{7,5},{8,10},{9,11},{10,... | collective-permute-start | bytes 860168 | tf_op jit(solution)/shard_map/ppermute | solution.py:258
  40.0 2.4 %collective-permute-start.15 = (bf16[112,1280]{1,0:T(8,128)(2,1)S(1)}, bf16[112,1280]{1,0:T(8,128)(2,1)S(1)}, u32[]{:S(2)}, u32[]{:S(2)}) collective-permute-start(bf16[112,1280]{1,0:T(8,128)(2,1)S(1)} %collective-permute-done.11.refs_3_), channel_id=1, source_target_pairs={{0,2},{1,3},{2,0},{3,1},{4,6},{5,7},{6,4},{7,5},{8,10},{9,11},{10,... | collective-permute-start | bytes 860168 | tf_op jit(solution)/shard_map/ppermute | solution.py:258
  40.4 2.0 %collective-permute-start.13 = (bf16[112,1280]{1,0:T(8,128)(2,1)S(1)}, bf16[112,1280]{1,0:T(8,128)(2,1)S(1)}, u32[]{:S(2)}, u32[]{:S(2)}) collective-permute-start(bf16[112,1280]{1,0:T(8,128)(2,1)S(1)} %collective-permute-done.9.refs_1_), channel_id=1, source_target_pairs={{0,2},{1,3},{2,0},{3,1},{4,6},{5,7},{6,4},{7,5},{8,10},{9,11},{10,... | collective-permute-start | bytes 860168 | tf_op jit(solution)/shard_map/ppermute | solution.py:258
  40.5 2.2 %collective-permute-start.14 = (bf16[112,1280]{1,0:T(8,128)(2,1)S(1)}, bf16[112,1280]{1,0:T(8,128)(2,1)S(1)}, u32[]{:S(2)}, u32[]{:S(2)}) collective-permute-start(bf16[112,1280]{1,0:T(8,128)(2,1)S(1)} %collective-permute-done.10.refs_2_), channel_id=1, source_target_pairs={{0,2},{1,3},{2,0},{3,1},{4,6},{5,7},{6,4},{7,5},{8,10},{9,11},{10,... | collective-permute-start | bytes 860168 | tf_op jit(solution)/shard_map/ppermute | solution.py:258

commit v3 on v2

v3 whole, which is shorter than its diff:
```python
import functools

import jax
import jax.numpy as jnp
from jax import lax
from jax.experimental import pallas as pl
from jax.experimental.pallas import tpu as pltpu
from jax.sharding import PartitionSpec as P


AXES = ("grp", "fsdp")
f32 = jnp.float32
bf16 = jnp.bfloat16
PIECES = 8
BATCH = 32


def turned(row, height):
    return jnp.transpose(jnp.broadcast_to(row.astype(f32), (height, row.shape[1])))


def matches(row, pool):
    ids = lax.broadcasted_iota(jnp.int32, (pool, row.shape[1]), 0)
    return (ids == row).astype(f32).astype(bf16)


def pack_kernel(order, weight_ref, *refs):
    outs, sem = refs[:-1], refs[-1]
    copies = []
    for k, (out, block) in enumerate(zip(outs, order())):
        height = out.shape[0]
        rows = pl.ds(pl.multiple_of(block * height, 16), height)
        copies.append(pltpu.make_async_copy(weight_ref.at[rows], out, sem.at[k]))
    for c in copies:
        c.start()
    for c in copies:
        c.wait()


def ends_of(counts_ref):
    cands = counts_ref.shape[1]
    along = lax.broadcasted_iota(jnp.int32, (cands, cands), 0)
    across = lax.broadcasted_iota(jnp.int32, (cands, cands), 1)
    return jnp.sum(jnp.where(along <= across, turned(counts_ref[...], cands), 0.0), axis=0, keepdims=True)


def first_of(ends, device, rows):
    return jnp.sum(jnp.where(ends <= (device * rows).astype(f32), 1.0, 0.0), axis=1, keepdims=True)


def batch_columns(lefts, first, factor):
    cands, pool = lefts.shape[1], factor.shape[1]
    ids = lax.broadcasted_iota(jnp.int32, (BATCH, cands), 1).astype(f32)
    rows = lax.broadcasted_iota(jnp.int32, (BATCH, cands), 0).astype(f32)
    left = jnp.sum(jnp.where(ids == first + rows, lefts.astype(f32), 0.0), axis=1, keepdims=True)
    places = lax.broadcasted_iota(jnp.int32, (BATCH, pool), 1).astype(f32)
    selector = jnp.where(places == left, 1.0, 0.0).astype(bf16)
    return across_dot(selector, factor).astype(bf16)


def across_dot(a, b):
    return lax.dot_general(a, b, (((1,), (1,)), ((), ())), preferred_element_type=f32)


def offer_kernel(tokens, index_ref, counts_ref, factor_ref, *refs):
    out_ref, a, sem = refs[-3:]
    copy = pltpu.make_async_copy(factor_ref, a, sem)
    copy.start()
    partner = lax.axis_index("grp") * lax.axis_size("fsdp") + 1 - lax.axis_index("fsdp")
    first = first_of(ends_of(counts_ref), partner, tokens)
    if len(refs) > 3:
        first = first + (refs[0][0] * BATCH).astype(f32)
    copy.wait()
    out_ref[...] = batch_columns(index_ref[0:1, :], first, a[...])


def offer(tokens, index, counts, factor_a, *turn):
    return pl.pallas_call(
        functools.partial(offer_kernel, tokens),
        in_specs=[vmem(), vmem(), hbm()] + [pl.BlockSpec(memory_space=pltpu.SMEM)] * len(turn),
        out_specs=vmem(),
        out_shape=jax.ShapeDtypeStruct((BATCH, factor_a.shape[0]), bf16),
        scratch_shapes=[pltpu.VMEM(factor_a.shape, bf16), pltpu.SemaphoreType.DMA],
        compiler_params=params(8),
        name="offer",
    )(index, counts, *in_hbm(factor_a), *turn)


def owners(ends, counts_ref, device, rows):
    begins = ends - counts_ref[...].astype(f32)
    position = (device * rows + lax.broadcasted_iota(jnp.int32, (rows, ends.shape[1]), 0)).astype(f32)
    return jnp.where((position >= begins) & (position < ends), 1.0, 0.0).astype(bf16)


def few_of(hot, first):
    ids = lax.broadcasted_iota(jnp.int32, (hot.shape[1], BATCH), 0).astype(f32)
    slots = lax.broadcasted_iota(jnp.int32, (hot.shape[1], BATCH), 1).astype(f32)
    return jnp.dot(hot, jnp.where(ids == first + slots, 1.0, 0.0).astype(bf16), preferred_element_type=f32)


def round_kernel(turn_ref, total_ref, cols_ref, index_ref, counts_ref, tokens_ref, factor_ref, out_ref, x, a, sem):
    fsdp = lax.axis_index("fsdp")
    device = lax.axis_index("grp") * lax.axis_size("fsdp") + fsdp
    rows, depth = x.shape[0], a.shape[0]
    copies = [pltpu.make_async_copy(tokens_ref, x, sem.at[0]), pltpu.make_async_copy(factor_ref, a, sem.at[1])]
    for c in copies:
        c.start()
    ends = ends_of(counts_ref)
    first = first_of(ends, device, rows) + (turn_ref[0] * BATCH).astype(f32)
    few = few_of(owners(ends, counts_ref, device, rows), first)
    for c in copies:
        c.wait()
    near = x[:, pl.ds(pl.multiple_of(fsdp * depth, 128), depth)]
    far = x[:, pl.ds(pl.multiple_of((1 - fsdp) * depth, 128), depth)]
    sc = across_dot(near, batch_columns(index_ref[0:1, :], first, a[...])) + across_dot(far, cols_ref[...])
    out_ref[...] = total_ref[...] + jnp.sum(few * sc, axis=1, keepdims=True)


def one_round(turn, total, cols, index, counts, tokens, factor_a):
    return pl.pallas_call(
        round_kernel,
        in_specs=[pl.BlockSpec(memory_space=pltpu.SMEM)] + [vmem()] * 4 + [hbm()] * 2,
        out_specs=vmem(),
        out_shape=jax.ShapeDtypeStruct(total.shape, f32),
        scratch_shapes=[
            pltpu.VMEM(tokens.shape, bf16), pltpu.VMEM(factor_a.shape, bf16), pltpu.SemaphoreType.DMA((2,)),
        ],
        compiler_params=params(16),
        name="round",
    )(turn, total, cols, index, counts, *in_hbm(tokens, factor_a))


def vmem():
    return pl.BlockSpec(memory_space=pltpu.VMEM)


def hbm():
    return pl.BlockSpec(memory_space=pltpu.HBM)


def in_hbm(*arrays):
    return [pltpu.with_memory_space_constraint(a, pltpu.HBM) for a in arrays]


def params(mib):
    return pltpu.CompilerParams(vmem_limit_bytes=mib << 20)


def pack(order, heights, weight):
    width = weight.shape[1]
    return pl.pallas_call(
        functools.partial(pack_kernel, order),
        in_specs=[hbm()],
        out_specs=[vmem()] * len(heights),
        out_shape=[jax.ShapeDtypeStruct((h, width), bf16) for h in heights],
        scratch_shapes=[pltpu.SemaphoreType.DMA((len(heights),))],
        compiler_params=params(4),
        name="pack",
    )(*in_hbm(weight))


def near_kernel(tokens_ref, weight_ref, target_ref, near_ref, far_ref, base_ref, w, t, sem):
    fsdp = lax.axis_index("fsdp")
    depth = far_ref.shape[1]
    near = pl.ds(pl.multiple_of(fsdp * depth, 128), depth)
    other = pl.ds(pl.multiple_of((1 - fsdp) * depth, 128), depth)
    pairs = [
        (tokens_ref.at[:, near], near_ref), (weight_ref, w), (target_ref, t), (tokens_ref.at[:, other], far_ref),
    ]
    copies = [pltpu.make_async_copy(s, d, sem.at[k]) for k, (s, d) in enumerate(pairs)]
    for c in copies:
        c.start()
    for c in copies[:3]:
        c.wait()
    base_ref[...] = jnp.dot(near_ref[...], w[...], preferred_element_type=f32) - t[...].astype(f32)
    copies[3].wait()


def near_half(tokens, weight, target):
    rows, width = target.shape
    depth = weight.shape[0]
    return pl.pallas_call(
        near_kernel,
        in_specs=[hbm()] * 3,
        out_specs=[vmem()] * 3,
        out_shape=[
            jax.ShapeDtypeStruct((rows, depth), bf16), jax.ShapeDtypeStruct((rows, depth), bf16),
            jax.ShapeDtypeStruct((rows, width), f32),
        ],
        scratch_shapes=[
            pltpu.VMEM((depth, width), bf16), pltpu.VMEM((rows, width), bf16), pltpu.SemaphoreType.DMA((4,)),
        ],
        compiler_params=params(14),
        cost_estimate=pl.CostEstimate(flops=8 * rows * depth * width, bytes_accessed=8 << 20, transcendentals=0),
        name="near",
    )(*in_hbm(tokens, weight, target))


def tables_kernel(
    index_ref, counts_ref, near_ref, factor_ref, rights_ref,
    sc_ref, hot_ref, few_ref, right_ref, columns_ref, chosen_ref, a, b, sem,
):
    device = lax.axis_index("grp") * lax.axis_size("fsdp") + lax.axis_index("fsdp")
    rows, pool = near_ref.shape[0], factor_ref.shape[1]
    copies = [pltpu.make_async_copy(s, d, sem.at[k]) for k, (s, d) in enumerate([(rights_ref, b), (factor_ref, a)])]
    for c in copies:
        c.start()
    ends = ends_of(counts_ref)
    first = first_of(ends, device, rows)
    hot = owners(ends, counts_ref, device, rows)
    hot_ref[...] = hot
    few_ref[...] = few_of(hot, first)
    copies[0].wait()
    chosen = lax.dot_general(
        matches(index_ref[1:2, :], pool), b[...], (((0,), (0,)), ((), ())), preferred_element_type=f32
    ).astype(bf16)
    chosen_ref[...] = chosen
    right_ref[...] = jnp.dot(hot, chosen, preferred_element_type=f32).astype(bf16)
    copies[1].wait()
    columns_ref[...] = jnp.dot(a[...], matches(index_ref[0:1, :], pool), preferred_element_type=f32).astype(bf16)
    sc_ref[...] = across_dot(near_ref[...], batch_columns(index_ref[0:1, :], first, a[...]))


def tables(index, counts, near, factor_a, factor_b):
    rows, depth = near.shape
    (pool, width), cands = factor_b.shape, counts.shape[1]

    def shaped(*shape, dtype=bf16):
        return jax.ShapeDtypeStruct(shape, dtype)

    return pl.pallas_call(
        tables_kernel,
        in_specs=[vmem()] * 3 + [hbm()] * 2,
        out_specs=[vmem()] * 6,
        out_shape=[
            shaped(rows, BATCH, dtype=f32), shaped(rows, cands), shaped(rows, BATCH, dtype=f32),
            shaped(rows, width), shaped(depth, cands), shaped(cands, width),
        ],
        scratch_shapes=[
            pltpu.VMEM((depth, pool), bf16), pltpu.VMEM((pool, width), bf16), pltpu.SemaphoreType.DMA((2,)),
        ],
        compiler_params=params(12),
        cost_estimate=pl.CostEstimate(flops=8 * rows * depth * width, bytes_accessed=4 << 20, transcendentals=0),
        name="tables",
    )(index, counts, near, *in_hbm(factor_a, factor_b))


def stack(pieces, blocks, held):
    height = pieces[0].shape[0]
    for piece, block in zip(pieces, blocks):
        held[pl.ds(pl.multiple_of(block * height, 16), height), :] = piece[...]


def middle_kernel(order, x_ref, base_ref, sc_ref, cols_ref, *refs):
    pieces, base_out, sc_out, held = refs[:-3], *refs[-3:]
    stack(pieces, order(), held)
    rows = base_ref.shape[0]
    half = held.shape[0]
    step = 128
    for r in range(0, rows, step):
        s = slice(r, r + step)
        acc = jnp.dot(x_ref[s, :half], held[...], preferred_element_type=f32)
        base_out[s, :] = base_ref[s, :] + acc
        sc_out[s, :] = sc_ref[s, :] + across_dot(x_ref[s, :], cols_ref[...])


def middle(order, x, base, sc, cols, pieces):
    depth, columns = x.shape[1], base.shape[1]
    return pl.pallas_call(
        functools.partial(middle_kernel, order),
        in_specs=[vmem()] * (4 + len(pieces)),
        out_specs=[vmem()] * 2,
        out_shape=[jax.ShapeDtypeStruct(base.shape, f32), jax.ShapeDtypeStruct(sc.shape, f32)],
        scratch_shapes=[pltpu.VMEM((sum(p.shape[0] for p in pieces), columns), bf16)],
        compiler_params=params(12),
        cost_estimate=pl.CostEstimate(
            flops=4 * x.shape[0] * depth * columns, bytes_accessed=4 << 20, transcendentals=0
        ),
        name="middle",
    )(x, base, sc, cols, *pieces)


def loss_kernel(noise, order, x_ref, base_ref, sc_ref, few_ref, more_ref, right_ref, hot_ref, *refs):
    pieces, out_ref, held = refs[:-2], refs[-2], refs[-1]
    stack(pieces, order(), held)
    rows, width = base_ref.shape
    half = held.shape[0]
    total = None
    step = 128
    for r in range(0, rows, step):
        s = slice(r, r + step)
        acc = jnp.dot(x_ref[s, x_ref.shape[1] - half :], held[...], preferred_element_type=f32)
        hot = hot_ref[s, :].astype(f32)
        picked = (jnp.sum(few_ref[s, :] * sc_ref[s, :], axis=1, keepdims=True) + more_ref[s, :]) * noise
        diff = acc + base_ref[s, :] + picked * right_ref[s, :].astype(f32)
        loss = jnp.sum(diff * diff, axis=1, keepdims=True) * (1.0 / width)
        part = jnp.sum(hot * loss, axis=0, keepdims=True)
        total = part if total is None else total + part
    out_ref[...] = jnp.broadcast_to(total[None], out_ref.shape)


def losses(noise, order, x, base, sc, few, more, right, hot, pieces, devices):
    width, cands = base.shape[1], hot.shape[1]
    return pl.pallas_call(
        functools.partial(loss_kernel, noise, order),
        in_specs=[vmem()] * (7 + len(pieces)),
        out_specs=vmem(),
        out_shape=jax.ShapeDtypeStruct((devices, 1, cands), f32),
        scratch_shapes=[pltpu.VMEM((sum(p.shape[0] for p in pieces), width), bf16)],
        compiler_params=params(12),
        name="losses",
    )(x, base, sc, few, more, right, hot, *pieces)


def update_kernel(step, parts_ref, counts_ref, columns_ref, chosen_ref, update_ref, scores_ref, held, sem):
    cands = counts_ref.shape[1]
    totals = jnp.sum(parts_ref[...], axis=0)
    fitness = -totals / counts_ref[...].astype(f32)
    middle = jnp.sum(fitness, axis=1, keepdims=True) / cands
    spread = jnp.sum((fitness - middle) ** 2, axis=1, keepdims=True) / cands
    scores = (fitness - middle) / jnp.sqrt(spread + 1e-06)
    scores_ref[...] = scores
    copies = []
    for k in range(columns_ref.shape[0] // step):
        s = pl.ds(k * step, step)
        scaled = (columns_ref[s, :].astype(f32) * scores).astype(bf16)
        held[s, :] = jnp.dot(scaled, chosen_ref[...], preferred_element_type=f32) * (1.0 / cands**0.5)
        c = pltpu.make_async_copy(held.at[s], update_ref.at[s], sem.at[k])
        c.start()
        copies.append(c)
    for c in copies:
        c.wait()


def update_of(parts, counts, columns, chosen):
    depth, cands = columns.shape
    width = chosen.shape[1]
    step = next(s for s in (128, 64, 32, 16, depth) if depth % s == 0)
    return pl.pallas_call(
        functools.partial(update_kernel, step),
        in_specs=[vmem()] * 4,
        out_specs=[hbm(), vmem()],
        out_shape=[jax.ShapeDtypeStruct((depth, width), f32), jax.ShapeDtypeStruct((1, cands), f32)],
        scratch_shapes=[pltpu.VMEM((depth, width), f32), pltpu.SemaphoreType.DMA((depth // step,))],
        compiler_params=params(12),
        name="update",
    )(parts, counts, columns, chosen)


def hop(value, bit, devices):
    return lax.ppermute(value, AXES, [(i, i ^ bit) for i in range(devices)])


def place():
    grp = lax.axis_index("grp")
    return jnp.bitwise_and(grp, 1), jnp.bitwise_and(jnp.right_shift(grp, 1), 3)


def sent():
    core, spot = place()
    return [2 * i + core for i in (spot, spot + 4, 3 - spot, 7 - spot)]


def further(rounds, index, counts, tokens, factor_a):
    rows, devices = tokens.shape[0], lax.axis_size("grp") * lax.axis_size("fsdp")

    def one(k, total):
        turn = jnp.full((1,), k, jnp.int32)
        theirs = hop(offer(rows, index, counts, factor_a, turn), 1, devices)
        return one_round(turn, total, theirs, index, counts, tokens, factor_a)

    return lax.fori_loop(1, rounds, one, jnp.zeros((rows, 1), f32))


def rounds_of(counts, rows, devices):
    ids = jnp.arange(counts.shape[0], dtype=jnp.int32)
    ends = jnp.sum(jnp.where(ids[:, None] <= ids[None, :], counts[:, None], 0), axis=0)
    starts = jnp.arange(devices, dtype=jnp.int32)[:, None] * rows
    inside = (ends[None, :] > starts) & ((ends - counts)[None, :] < starts + rows)
    most = jnp.max(jnp.sum(inside.astype(jnp.int32), axis=1))
    return (most + BATCH - 1) // BATCH


def arrived():
    core, spot = place()
    ids = [spot, jnp.bitwise_xor(spot, 1), jnp.bitwise_xor(spot, 2), 3 - spot]
    return [2 * i + core for i in ids] + [2 * i + 1 - core for i in ids]


def per_device(groups, parts, tokens, target, weight, factor_a, factor_b, counts, cand_index):
    return compute(groups, parts, tokens, target, weight, factor_a, factor_b, counts, cand_index)


def compute(groups, parts, tokens, target, weight, factor_a, factor_b, counts, cand_index):
    devices = groups * parts
    rows, full = tokens.shape
    depth = weight.shape[0]
    cands = counts.shape[0]
    noise = 0.5 * full ** (-0.5)
    index = cand_index.T
    if parts == 2 and groups % 8 == 0 and depth % (2 * PIECES * 16) == 0:
        height = depth // (2 * PIECES)
        first, second, third, fourth = pack(sent, [height] * 4, weight)
        given = offer(rows, index, counts[None, :], factor_a)
        more = further(rounds_of(counts, rows, devices), index, counts[None, :], tokens, factor_a)
        y1, y2 = hop(first, 1, devices), hop(second, 1, devices)
        y3, y4 = hop(third, 1, devices), hop(fourth, 1, devices)
        taken = hop(given, 1, devices)
        x1, z1 = hop(y1, 4, devices), hop(y1, 8, devices)
        x2, z2 = hop(y2, 4, devices), hop(y2, 8, devices)
        early, late = {"y1": y1, "x1": x1, "z1": z1, "y3": y3}, {"y2": y2, "x2": x2, "z2": z2, "y4": y4}
        early, late = (
            [*some.values()] + [hop(v, 2, devices) for v in some.values()] for some in (early, late)
        )
        near, far, base = near_half(tokens, weight, target)
        sc, hot, few, right_rows, columns, chosen = tables(index, counts[None, :], near, factor_a, factor_b)
        base, sc = middle(arrived, far, base, sc, taken, early)
        sums = losses(noise, arrived, far, base, sc, few, more, right_rows, hot, late, devices)
    else:
        left, right = cand_index[:, 0], cand_index[:, 1]
        cand_ids = jnp.arange(cands, dtype=jnp.int32)
        ends = jnp.sum(jnp.where(cand_ids[:, None] <= cand_ids[None, :], counts[:, None], 0), axis=0)
        position = lax.axis_index(AXES) * rows + jnp.arange(rows, dtype=jnp.int32)
        hot = (position[:, None] >= (ends - counts)[None, :]) & (position[:, None] < ends[None, :])
        owned = hot.astype(f32)
        columns = jnp.take(factor_a, left, axis=1)
        chosen = jnp.take(factor_b, right, axis=0)
        right_rows = jnp.dot(hot.astype(bf16), chosen, preferred_element_type=f32)
        all_weight = lax.all_gather(weight, "fsdp", axis=0, tiled=True)
        all_columns = lax.all_gather(columns, "fsdp", axis=0, tiled=True)
        base = jnp.dot(tokens, all_weight, preferred_element_type=f32)
        sc = jnp.dot(tokens, all_columns, preferred_element_type=f32)
        picked = noise * jnp.sum(owned * sc, axis=1)
        diff = base + picked[:, None] * right_rows - target.astype(f32)
        loss = jnp.mean(diff * diff, axis=1)
        sums = jnp.broadcast_to(jnp.sum(owned * loss[:, None], axis=0)[None, None, :], (devices, 1, cands))
    spread = lax.all_to_all(sums, AXES, split_axis=0, concat_axis=0, tiled=True)
    update, scores = update_of(spread, counts[None, :], columns, chosen)
    return update, scores[0]


def solution(mesh):
    in_specs = (
        P(AXES, None),
        P(AXES, None),
        P("fsdp", None),
        P("fsdp", None),
        P(),
        P(),
        P(),
    )
    return jax.shard_map(
        functools.partial(per_device, mesh.shape["grp"], mesh.shape["fsdp"]),
        mesh=mesh,
        in_specs=in_specs,
        out_specs=(P("fsdp", None), P()),
        check_vma=False,
    )
```

time: 59.8 us -> 75.8 us (1.27)
  local copies, waits for them, and re-layouts: 0.01 us -> 23.1 us
  waiting for transfers between devices: 18.3 us -> 2.61 us
  Pallas kernels: 15.8 us -> 20.7 us
  starting transfers between devices: 13.7 us -> 15 us
  other arithmetic: 0 us -> 0.95 us
  between operations: 0.73 us -> 1.49 us
    unnamed x4 -> x64, local copies, waits for them, and re-layouts: 0.01 us -> 22.4 us
    ppermute x16 -> x17, waiting for transfers between devices: 18.3 us -> 2.61 us  [hop(): return lax.ppermute(value, AXES, [(i, i ^ bit) for i in range(devices)])]
    pallas_call x3 -> x4, Pallas kernels: 8.56 us -> 12.1 us  [the longest x1 4.26 us: near_half(): pl.pallas_call(near_kernel, in_specs=[hbm()] * 3, out_specs=[vmem()] * 3,...]
    ppermute x16 -> x17, starting transfers between devices: 13.7 us -> 15 us  [hop(): return lax.ppermute(value, AXES, [(i, i ^ bit) for i in range(devices)])]
    pallas_call x1, Pallas kernels: 1.78 us -> 2.99 us  [losses(): pl.pallas_call(functools.partial(loss_kernel, noise, order), in_specs=[vm...]
  transfers between devices with their start and end apart: 16 -> 17, of which waited for: 5 -> 3; matrix products, arithmetic and copies ran while one was open for 0% -> 2% of each run, Pallas kernels for 15% -> 14%
where the time goes in v3:
time: 75.8 us; the launch traced here: 75.1 us
  local copies, waits for them, and re-layouts  23.1 us (30%)
  Pallas kernels  20.7 us (27%)
  starting transfers between devices  15 us (20%)
  blocking collectives  11.3 us (15%)
  waiting for transfers between devices  2.61 us (3%)
  between operations  1.49 us (2%)
  other arithmetic  0.95 us (1%)
    unnamed x64, local copies, waits for them, and re-layouts  22.4 us
    ppermute x17, starting transfers between devices, hop(): return lax.ppermute(value, AXES, [(i, i ^ bit) for i in range(devices)])  15 us
    all_to_all x1, blocking collectives, compute(): spread = lax.all_to_all(sums, AXES, split_axis=0, concat_axis=0, tiled=True)  11.3 us
    pallas_call x1, Pallas kernels, near_half(): pl.pallas_call(near_kernel, in_specs=[hbm()] * 3, out_specs=[vmem()] * 3,...  4.26 us
    pallas_call x1, Pallas kernels, update_of(): pl.pallas_call(functools.partial(update_kernel, step), in_specs=[vmem()]...  4.07 us
    pallas_call x1, Pallas kernels, tables(): pl.pallas_call(tables_kernel, in_specs=[vmem()] * 3 + [hbm()] * 2, out_sp...  3.71 us
    pallas_call x1, Pallas kernels, losses(): pl.pallas_call(functools.partial(loss_kernel, noise, order), in_specs=[vm...  2.99 us
    pallas_call x1, Pallas kernels, offer(): pl.pallas_call(functools.partial(offer_kernel, tokens), in_specs=[vmem(),...  2.86 us
  transfers between devices with their start and end apart: 17, of which 3 were waited for; matrix products, arithmetic and copies ran while one was open for 2% of the time, Pallas kernels for 14%

profile of v3, /device:TPU:0, one launch (start us, length us, event | category | flops | bytes accessed | tf_op | source)
XLA Modules:
  0.0 75.1 jit_solution(5456735261982164199)
XLA Ops:
  0.6 2.9 %offer.2 = bf16[32,1792]{1,0:T(8,128)(2,1)S(1)} custom-call(s32[2,256]{1,0:T(2,128)} %bitcast.6, s32[1,256]{1,0:T(1,128)} %bitcast.9, bf16[1792,512]{1,0:T(8,128)(2,1)} %factor_ref.3), custom_call_target="tpu_custom_call" | custom-call | tf_op jit(solution)/shard_map/offer/pallas_call | solution.py:78
  3.5 3.1 %collective-permute-start.1 = (bf16[32,1792]{1,0:T(8,128)(2,1)S(1)}, bf16[32,1792]{1,0:T(8,128)(2,1)S(1)}, u32[]{:S(2)}, u32[]{:S(2)}) collective-permute-start(bf16[32,1792]{1,0:T(8,128)(2,1)S(1)} %offer.2), channel_id=1, source_target_pairs={{0,1},{1,0},{2,3},{3,2},{4,5},{5,4},{6,7},{7,6},{8,9},{9,8},{10,11... | collective-permute-start | bytes 344072 | tf_op jit(solution)/shard_map/ppermute | solution.py:351
  6.6 1.3 %pack.1 = (bf16[112,1024]{1,0:T(8,128)(2,1)S(1)}, bf16[112,1024]{1,0:T(8,128)(2,1)S(1)}, bf16[112,1024]{1,0:T(8,128)(2,1)S(1)}, bf16[112,1024]{1,0:T(8,128)(2,1)S(1)}) custom-call(bf16[1792,1024]{1,0:T(8,128)(2,1)} %weight_ref.3), custom_call_target="tpu_custom_call" | custom-call | tf_op jit(solution)/shard_map/pack/pallas_call | solution.py:151
  8.0 2.0 %collective-permute-start.5 = (bf16[112,1024]{1,0:T(8,128)(2,1)S(1)}, bf16[112,1024]{1,0:T(8,128)(2,1)S(1)}, u32[]{:S(2)}, u32[]{:S(2)}) collective-permute-start(bf16[112,1024]{1,0:T(8,128)(2,1)S(1)} %get-tuple-element.62), channel_id=1, source_target_pairs={{0,1},{1,0},{2,3},{3,2},{4,5},{5,4},{6,7},{7,6},{8,9},{9,8},{10,11... | collective-permute-start | bytes 688136 | tf_op jit(solution)/shard_map/ppermute | solution.py:351
  10.1 4.3 %near.1 = (bf16[384,1792]{1,0:T(8,128)(2,1)S(1)}, bf16[384,1792]{1,0:T(8,128)(2,1)S(1)}, f32[384,1024]{1,0:T(8,128)S(1)}) custom-call(bf16[384,3584]{1,0:T(8,128)(2,1)} %tokens_ref.1, bf16[1792,1024]{1,0:T(8,128)(2,1)} %weight_ref.3, bf16[384,1024]{1,0:T(8,128)(2,1)} %target_ref.1), custom_call_target="tpu_custom_call" | custom-call | flops 5637144576 | bytes 8388608 | tf_op jit(solution)/shard_map/near/pallas_call | solution.py:182
  14.3 2.0 %collective-permute-start.13 = (bf16[112,1024]{1,0:T(8,128)(2,1)S(1)}, bf16[112,1024]{1,0:T(8,128)(2,1)}, u32[]{:S(2)}, u32[]{:S(2)}) collective-permute-start(bf16[112,1024]{1,0:T(8,128)(2,1)S(1)} %get-tuple-element.70), channel_id=1, source_target_pairs={{0,1},{1,0},{2,3},{3,2},{4,5},{5,4},{6,7},{7,6},{8,9},{9,8},{10,11... | collective-permute-start | bytes 688136 | tf_op jit(solution)/shard_map/ppermute | solution.py:351
  16.4 1.5 %collective-permute-start.3 = (bf16[112,1024]{1,0:T(8,128)(2,1)S(1)}, bf16[112,1024]{1,0:T(8,128)(2,1)S(1)}, u32[]{:S(2)}, u32[]{:S(2)}) collective-permute-start(bf16[112,1024]{1,0:T(8,128)(2,1)S(1)} %collective-permute-done.2.refs_0_), channel_id=1, source_target_pairs={{0,4},{1,5},{2,6},{3,7},{4,0},{5,1},{6,2},{7,3},{8,12},{9,13},{10,... | collective-permute-start | bytes 688136 | tf_op jit(solution)/shard_map/ppermute | solution.py:351
  17.9 1.6 %collective-permute-start.4 = (bf16[112,1024]{1,0:T(8,128)(2,1)S(1)}, bf16[112,1024]{1,0:T(8,128)(2,1)S(1)}, u32[]{:S(2)}, u32[]{:S(2)}) collective-permute-start(bf16[112,1024]{1,0:T(8,128)(2,1)S(1)} %collective-permute-done.2.refs_0_), channel_id=1, source_target_pairs={{0,8},{1,9},{2,10},{3,11},{4,12},{5,13},{6,14},{7,15},{8,0},{9,1},... | collective-permute-start | bytes 688136 | tf_op jit(solution)/shard_map/ppermute | solution.py:351
  19.5 1.8 %collective-permute-done.5.refs_3_ = bf16[112,1024]{1,0:T(8,128)(2,1)S(1)} collective-permute-done((bf16[112,1024]{1,0:T(8,128)(2,1)S(1)}, bf16[112,1024]{1,0:T(8,128)(2,1)S(1)}, u32[]{:S(2)}, u32[]{:S(2)}) %collective-permute-start.5) | collective-permute-done | bytes 229408 | tf_op jit(solution)/shard_map/ppermute | solution.py:351
  21.4 3.7 %tables.1 = (f32[384,32]{1,0:T(8,128)S(1)}, bf16[384,256]{1,0:T(8,128)(2,1)S(1)}, f32[384,32]{1,0:T(8,128)S(1)}, bf16[384,1024]{1,0:T(8,128)(2,1)S(1)}, bf16[179...) custom-call(s32[2,256]{1,0:T(2,128)S(1)} %bitcast.7, s32[1,256]{1,0:T(1,128)S(1)} %bitcast.10, ...), custom_call_target="tpu_custom_call" | custom-call | flops 5637144576 | bytes 4194304 | tf_op jit(solution)/shard_map/tables/pallas_call | solution.py:231
  29.7 1.5 %collective-permute-start.11 = (bf16[112,1024]{1,0:T(8,128)(2,1)S(1)}, bf16[112,1024]{1,0:T(8,128)(2,1)}, u32[]{:S(2)}, u32[]{:S(2)}) collective-permute-start(bf16[112,1024]{1,0:T(8,128)(2,1)S(1)} %collective-permute-done.10.refs_0_), channel_id=1, source_target_pairs={{0,4},{1,5},{2,6},{3,7},{4,0},{5,1},{6,2},{7,3},{8,12},{9,13},{10,... | collective-permute-start | bytes 688136 | tf_op jit(solution)/shard_map/ppermute | solution.py:351
  31.2 1.6 %collective-permute-start.12 = (bf16[112,1024]{1,0:T(8,128)(2,1)S(1)}, bf16[112,1024]{1,0:T(8,128)(2,1)}, u32[]{:S(2)}, u32[]{:S(2)}) collective-permute-start(bf16[112,1024]{1,0:T(8,128)(2,1)S(1)} %collective-permute-done.10.refs_0_), channel_id=1, source_target_pairs={{0,8},{1,9},{2,10},{3,11},{4,12},{5,13},{6,14},{7,15},{8,0},{9,1},... | collective-permute-start | bytes 688136 | tf_op jit(solution)/shard_map/ppermute | solution.py:351
  41.0 0.9 %copy-done.13 = bf16[112,1024]{1,0:T(8,128)(2,1)S(1)} copy-done((bf16[112,1024]{1,0:T(8,128)(2,1)S(1)}, bf16[112,1024]{1,0:T(8,128)(2,1)}, u32[]{:S(2)}) %copy-start.13) | copy-done | bytes 229400
  41.9 0.9 %copy-done.15 = bf16[112,1024]{1,0:T(8,128)(2,1)S(1)} copy-done((bf16[112,1024]{1,0:T(8,128)(2,1)S(1)}, bf16[112,1024]{1,0:T(8,128)(2,1)}, u32[]{:S(2)}) %copy-start.15) | copy-done | bytes 229400
  42.8 0.9 %copy-done.17 = bf16[112,1024]{1,0:T(8,128)(2,1)S(1)} copy-done((bf16[112,1024]{1,0:T(8,128)(2,1)S(1)}, bf16[112,1024]{1,0:T(8,128)(2,1)}, u32[]{:S(2)}) %copy-start.17) | copy-done | bytes 229400
  44.7 0.9 %copy-done.21 = bf16[112,1024]{1,0:T(8,128)(2,1)S(1)} copy-done((bf16[112,1024]{1,0:T(8,128)(2,1)S(1)}, bf16[112,1024]{1,0:T(8,128)(2,1)}, u32[]{:S(2)}) %copy-start.21) | copy-done | bytes 229400
  45.7 0.9 %copy-done.23 = bf16[112,1024]{1,0:T(8,128)(2,1)S(1)} copy-done((bf16[112,1024]{1,0:T(8,128)(2,1)S(1)}, bf16[112,1024]{1,0:T(8,128)(2,1)}, u32[]{:S(2)}) %copy-start.23) | copy-done | bytes 229400
  46.6 0.9 %copy-done.25 = bf16[112,1024]{1,0:T(8,128)(2,1)S(1)} copy-done((bf16[112,1024]{1,0:T(8,128)(2,1)S(1)}, bf16[112,1024]{1,0:T(8,128)(2,1)}, u32[]{:S(2)}) %copy-start.25) | copy-done | bytes 229400
  47.5 1.4 %copy-done.27 = f32[384,1024]{1,0:T(8,128)S(1)} copy-done((f32[384,1024]{1,0:T(8,128)S(1)}, f32[384,1024]{1,0:T(8,128)}, u32[]{:S(2)}) %copy-start.27) | copy-done | bytes 1572888
  49.9 1.5 %middle.1 = (f32[384,1024]{1,0:T(8,128)S(1)}, f32[384,32]{1,0:T(8,128)S(1)}) custom-call(bf16[384,1792]{1,0:T(8,128)(2,1)S(1)} %get-tuple-element.57.x_ref, f32[384,1024]{1,0:T(8,128)S(1)} %copy-done.27, f32[384,32]{1,0:T(8,128)S(1)} %copy-done.29, bf16[32,1792]{1,0:T(8,128)(2,1)S(1)} %collective-permute-done.1.cols_ref, ...), custom_call_target="tpu_custom_call" | custom-call | flops 2818572288 | bytes 4194304 | tf_op jit(solution)/shard_map/middle/pallas_call | solution.py:269
  52.8 1.1 %copy-done.3 = bf16[384,1024]{1,0:T(8,128)(2,1)S(1)} copy-done((bf16[384,1024]{1,0:T(8,128)(2,1)S(1)}, bf16[384,1024]{1,0:T(8,128)(2,1)}, u32[]{:S(2)}) %copy-start.3) | copy-done | bytes 786456
  56.7 3.0 %losses.1 = f32[32,1,256]{2,1,0:T(1,128)S(1)} custom-call(bf16[384,1792]{1,0:T(8,128)(2,1)S(1)} %get-tuple-element.57.x_ref, f32[384,1024]{1,0:T(8,128)S(1)} %get-tuple-element.63.base_ref, f32[384,32]{1,0:T(8,128)S(1)} %copy-done.11, f32[384,32]{1,0:T(8,128)S(1)} %copy-done.9, f32[384,1]{1,0:T(8,128)} %get-tuple-element.66.more_ref, ...), custom_call_target="tpu_custom_call" | custom-call | tf_op jit(solution)/shard_map/losses/pallas_call | solution.py:304
  59.7 11.3 %all_to_all.5.parts_ref = f32[32,1,256]{2,1,0:T(1,128)S(1)} all-to-all(f32[32,1,256]{2,1,0:T(1,128)S(1)} %losses.1), channel_id=1, replica_groups=mesh['grp'=16,'fsdp'=2] {'grp','fsdp'}, dimensions={0} | all-to-all | bytes 65536 | tf_op jit(solution)/shard_map/all_to_all | solution.py:437
  71.0 4.1 %update.1 = (f32[1792,1024]{1,0:T(8,128)}, f32[1,256]{1,0:T(1,128)}) custom-call(f32[32,1,256]{2,1,0:T(1,128)S(1)} %all_to_all.5.parts_ref, s32[1,256]{1,0:T(1,128)S(1)} %get-tuple-element.185, bf16[1792,256]{1,0:T(8,128)(2,1)S(1)} %copy-done.1, bf16[256,1024]{1,0:T(8,128)(2,1)S(1)} %copy-done.5), custom_call_target="tpu_custom_call" | custom-call | tf_op jit(solution)/shard_map/update/pallas_call | solution.py:339
  (89 shorter events, 18.4 us)
Async XLA Ops:
  3.5 14.4 %collective-permute-start.1 = (bf16[32,1792]{1,0:T(8,128)(2,1)S(1)}, bf16[32,1792]{1,0:T(8,128)(2,1)S(1)}, u32[]{:S(2)}, u32[]{:S(2)}) collective-permute-start(bf16[32,1792]{1,0:T(8,128)(2,1)S(1)} %offer.2), channel_id=1, source_target_pairs={{0,1},{1,0},{2,3},{3,2},{4,5},{5,4},{6,7},{7,6},{8,9},{9,8},{10,11... | collective-permute-start | bytes 344072 | tf_op jit(solution)/shard_map/ppermute | solution.py:351
  7.9 8.5 %collective-permute-start.2 = (bf16[112,1024]{1,0:T(8,128)(2,1)S(1)}, bf16[112,1024]{1,0:T(8,128)(2,1)S(1)}, u32[]{:S(2)}, u32[]{:S(2)}) collective-permute-start(bf16[112,1024]{1,0:T(8,128)(2,1)S(1)} %get-tuple-element.61), channel_id=1, source_target_pairs={{0,1},{1,0},{2,3},{3,2},{4,5},{5,4},{6,7},{7,6},{8,9},{9,8},{10,11... | collective-permute-start | bytes 688136 | tf_op jit(solution)/shard_map/ppermute | solution.py:351
  8.0 13.4 %collective-permute-start.5 = (bf16[112,1024]{1,0:T(8,128)(2,1)S(1)}, bf16[112,1024]{1,0:T(8,128)(2,1)S(1)}, u32[]{:S(2)}, u32[]{:S(2)}) collective-permute-start(bf16[112,1024]{1,0:T(8,128)(2,1)S(1)} %get-tuple-element.62), channel_id=1, source_target_pairs={{0,1},{1,0},{2,3},{3,2},{4,5},{5,4},{6,7},{7,6},{8,9},{9,8},{10,11... | collective-permute-start | bytes 688136 | tf_op jit(solution)/shard_map/ppermute | solution.py:351
  10.0 11.4 %copy-start.30 = (s32[256,2]{0,1:T(2,128)S(1)}, s32[256,2]{0,1:T(2,128)}, u32[]{:S(2)}) copy-start(s32[256,2]{0,1:T(2,128)} %param.15) | copy-start | bytes 6148
  10.0 11.4 %copy-start.31 = (s32[256]{0:T(256)S(1)}, s32[256]{0:T(256)}, u32[]{:S(2)}) copy-start(s32[256]{0:T(256)} %param.14) | copy-start | bytes 3076
  10.0 19.7 %collective-permute-start.10 = (bf16[112,1024]{1,0:T(8,128)(2,1)S(1)}, bf16[112,1024]{1,0:T(8,128)(2,1)S(1)}, u32[]{:S(2)}, u32[]{:S(2)}) collective-permute-start(bf16[112,1024]{1,0:T(8,128)(2,1)S(1)} %get-tuple-element.69), channel_id=1, source_target_pairs={{0,1},{1,0},{2,3},{3,2},{4,5},{5,4},{6,7},{7,6},{8,9},{9,8},{10,11... | collective-permute-start | bytes 688136 | tf_op jit(solution)/shard_map/ppermute | solution.py:351
  14.3 10.7 %copy-start.26 = (f32[384,1024]{1,0:T(8,128)}, f32[384,1024]{1,0:T(8,128)S(1)}, u32[]{:S(2)}) copy-start(f32[384,1024]{1,0:T(8,128)S(1)} %get-tuple-element.58.base_ref) | copy-start | bytes 4718596
  14.3 16.9 %collective-permute-start.13 = (bf16[112,1024]{1,0:T(8,128)(2,1)S(1)}, bf16[112,1024]{1,0:T(8,128)(2,1)}, u32[]{:S(2)}, u32[]{:S(2)}) collective-permute-start(bf16[112,1024]{1,0:T(8,128)(2,1)S(1)} %get-tuple-element.70), channel_id=1, source_target_pairs={{0,1},{1,0},{2,3},{3,2},{4,5},{5,4},{6,7},{7,6},{8,9},{9,8},{10,11... | collective-permute-start | bytes 688136 | tf_op jit(solution)/shard_map/ppermute | solution.py:351
  16.4 16.4 %collective-permute-start.3 = (bf16[112,1024]{1,0:T(8,128)(2,1)S(1)}, bf16[112,1024]{1,0:T(8,128)(2,1)S(1)}, u32[]{:S(2)}, u32[]{:S(2)}) collective-permute-start(bf16[112,1024]{1,0:T(8,128)(2,1)S(1)} %collective-permute-done.2.refs_0_), channel_id=1, source_target_pairs={{0,4},{1,5},{2,6},{3,7},{4,0},{5,1},{6,2},{7,3},{8,12},{9,13},{10,... | collective-permute-start | bytes 688136 | tf_op jit(solution)/shard_map/ppermute | solution.py:351
  17.9 14.9 %collective-permute-start.4 = (bf16[112,1024]{1,0:T(8,128)(2,1)S(1)}, bf16[112,1024]{1,0:T(8,128)(2,1)S(1)}, u32[]{:S(2)}, u32[]{:S(2)}) collective-permute-start(bf16[112,1024]{1,0:T(8,128)(2,1)S(1)} %collective-permute-done.2.refs_0_), channel_id=1, source_target_pairs={{0,8},{1,9},{2,10},{3,11},{4,12},{5,13},{6,14},{7,15},{8,0},{9,1},... | collective-permute-start | bytes 688136 | tf_op jit(solution)/shard_map/ppermute | solution.py:351
  21.3 11.5 %copy-start.12 = (bf16[112,1024]{1,0:T(8,128)(2,1)}, bf16[112,1024]{1,0:T(8,128)(2,1)S(1)}, u32[]{:S(2)}) copy-start(bf16[112,1024]{1,0:T(8,128)(2,1)S(1)} %collective-permute-done.5.refs_3_) | copy-start | bytes 688132
  21.3 12.7 %collective-permute-start.6 = (bf16[112,1024]{1,0:T(8,128)(2,1)S(1)}, bf16[112,1024]{1,0:T(8,128)(2,1)S(1)}, u32[]{:S(2)}, u32[]{:S(2)}) collective-permute-start(bf16[112,1024]{1,0:T(8,128)(2,1)S(1)} %collective-permute-done.2.refs_0_), channel_id=1, source_target_pairs={{0,2},{1,3},{2,0},{3,1},{4,6},{5,7},{6,4},{7,5},{8,10},{9,11},{10,... | collective-permute-start | bytes 688136 | tf_op jit(solution)/shard_map/ppermute | solution.py:351
  29.7 8.6 %collective-permute-start.11 = (bf16[112,1024]{1,0:T(8,128)(2,1)S(1)}, bf16[112,1024]{1,0:T(8,128)(2,1)}, u32[]{:S(2)}, u32[]{:S(2)}) collective-permute-start(bf16[112,1024]{1,0:T(8,128)(2,1)S(1)} %collective-permute-done.10.refs_0_), channel_id=1, source_target_pairs={{0,4},{1,5},{2,6},{3,7},{4,0},{5,1},{6,2},{7,3},{8,12},{9,13},{10,... | collective-permute-start | bytes 688136 | tf_op jit(solution)/shard_map/ppermute | solution.py:351
  31.2 7.8 %collective-permute-start.12 = (bf16[112,1024]{1,0:T(8,128)(2,1)S(1)}, bf16[112,1024]{1,0:T(8,128)(2,1)}, u32[]{:S(2)}, u32[]{:S(2)}) collective-permute-start(bf16[112,1024]{1,0:T(8,128)(2,1)S(1)} %collective-permute-done.10.refs_0_), channel_id=1, source_target_pairs={{0,8},{1,9},{2,10},{3,11},{4,12},{5,13},{6,14},{7,15},{8,0},{9,1},... | collective-permute-start | bytes 688136 | tf_op jit(solution)/shard_map/ppermute | solution.py:351
  32.8 4.4 %collective-permute-start.9 = (bf16[112,1024]{1,0:T(8,128)(2,1)S(1)}, bf16[112,1024]{1,0:T(8,128)(2,1)S(1)}, u32[]{:S(2)}, u32[]{:S(2)}) collective-permute-start(bf16[112,1024]{1,0:T(8,128)(2,1)S(1)} %collective-permute-done.5.refs_3_), channel_id=1, source_target_pairs={{0,2},{1,3},{2,0},{3,1},{4,6},{5,7},{6,4},{7,5},{8,10},{9,11},{10,... | collective-permute-start | bytes 688136 | tf_op jit(solution)/shard_map/ppermute | solution.py:351
  32.8 6.2 %collective-permute-start.7 = (bf16[112,1024]{1,0:T(8,128)(2,1)S(1)}, bf16[112,1024]{1,0:T(8,128)(2,1)S(1)}, u32[]{:S(2)}, u32[]{:S(2)}) collective-permute-start(bf16[112,1024]{1,0:T(8,128)(2,1)S(1)} %collective-permute-done.3.refs_1_), channel_id=1, source_target_pairs={{0,2},{1,3},{2,0},{3,1},{4,6},{5,7},{6,4},{7,5},{8,10},{9,11},{10,... | collective-permute-start | bytes 688136 | tf_op jit(solution)/shard_map/ppermute | solution.py:351
  34.8 5.5 %collective-permute-start.8 = (bf16[112,1024]{1,0:T(8,128)(2,1)S(1)}, bf16[112,1024]{1,0:T(8,128)(2,1)S(1)}, u32[]{:S(2)}, u32[]{:S(2)}) collective-permute-start(bf16[112,1024]{1,0:T(8,128)(2,1)S(1)} %collective-permute-done.4.refs_2_), channel_id=1, source_target_pairs={{0,2},{1,3},{2,0},{3,1},{4,6},{5,7},{6,4},{7,5},{8,10},{9,11},{10,... | collective-permute-start | bytes 688136 | tf_op jit(solution)/shard_map/ppermute | solution.py:351
  37.9 14.9 %collective-permute-start.14 = (bf16[112,1024]{1,0:T(8,128)(2,1)S(1)}, bf16[112,1024]{1,0:T(8,128)(2,1)}, u32[]{:S(2)}, u32[]{:S(2)}) collective-permute-start(bf16[112,1024]{1,0:T(8,128)(2,1)S(1)} %collective-permute-done.10.refs_0_), channel_id=1, source_target_pairs={{0,2},{1,3},{2,0},{3,1},{4,6},{5,7},{6,4},{7,5},{8,10},{9,11},{10,... | collective-permute-start | bytes 688136 | tf_op jit(solution)/shard_map/ppermute | solution.py:351
  38.3 14.4 %collective-permute-start.17 = (bf16[112,1024]{1,0:T(8,128)(2,1)}, bf16[112,1024]{1,0:T(8,128)(2,1)}, u32[]{:S(2)}, u32[]{:S(2)}) collective-permute-start(bf16[112,1024]{1,0:T(8,128)(2,1)} %collective-permute-done.13.refs_3_), channel_id=1, source_target_pairs={{0,2},{1,3},{2,0},{3,1},{4,6},{5,7},{6,4},{7,5},{8,10},{9,11},{10,... | collective-permute-start | bytes 688136 | tf_op jit(solution)/shard_map/ppermute | solution.py:351
  39.0 13.7 %collective-permute-start.15 = (bf16[112,1024]{1,0:T(8,128)(2,1)}, bf16[112,1024]{1,0:T(8,128)(2,1)}, u32[]{:S(2)}, u32[]{:S(2)}) collective-permute-start(bf16[112,1024]{1,0:T(8,128)(2,1)} %collective-permute-done.11.refs_1_), channel_id=1, source_target_pairs={{0,2},{1,3},{2,0},{3,1},{4,6},{5,7},{6,4},{7,5},{8,10},{9,11},{10,... | collective-permute-start | bytes 688136 | tf_op jit(solution)/shard_map/ppermute | solution.py:351
  39.8 13.0 %collective-permute-start.16 = (bf16[112,1024]{1,0:T(8,128)(2,1)}, bf16[112,1024]{1,0:T(8,128)(2,1)}, u32[]{:S(2)}, u32[]{:S(2)}) collective-permute-start(bf16[112,1024]{1,0:T(8,128)(2,1)} %collective-permute-done.12.refs_2_), channel_id=1, source_target_pairs={{0,2},{1,3},{2,0},{3,1},{4,6},{5,7},{6,4},{7,5},{8,10},{9,11},{10,... | collective-permute-start | bytes 688136 | tf_op jit(solution)/shard_map/ppermute | solution.py:351
  47.5 1.4 %copy-start.27 = (f32[384,1024]{1,0:T(8,128)S(1)}, f32[384,1024]{1,0:T(8,128)}, u32[]{:S(2)}) copy-start(f32[384,1024]{1,0:T(8,128)} %copy-done.26) | copy-start | bytes 4718596
  56.7 14.3 %copy-start.1 = (bf16[1792,256]{1,0:T(8,128)(2,1)S(1)}, bf16[1792,256]{1,0:T(8,128)(2,1)}, u32[]{:S(2)}) copy-start(bf16[1792,256]{1,0:T(8,128)(2,1)} %copy-done) | copy-start | bytes 2752516
  56.7 14.3 %copy-start.5 = (bf16[256,1024]{1,0:T(8,128)(2,1)S(1)}, bf16[256,1024]{1,0:T(8,128)(2,1)}, u32[]{:S(2)}) copy-start(bf16[256,1024]{1,0:T(8,128)(2,1)} %copy-done.4) | copy-start | bytes 1572868
  (25 other events, 21.0 us)

commit v4 on v3

--- a/solution.py
+++ b/solution.py
@@ -13,6 +13,7 @@
 bf16 = jnp.bfloat16
 PIECES = 8
 BATCH = 32
+CUT = 640
 
 
 def turned(row, height):
@@ -159,90 +160,91 @@
     )(*in_hbm(weight))
 
 
-def near_kernel(tokens_ref, weight_ref, target_ref, near_ref, far_ref, base_ref, w, t, sem):
+def near_kernel(
+    tokens_ref, weight_ref, target_ref, factor_ref, rights_ref, near_ref, far_ref, base_ref, a_ref, b_ref, w, t, sem
+):
     fsdp = lax.axis_index("fsdp")
     depth = far_ref.shape[1]
     near = pl.ds(pl.multiple_of(fsdp * depth, 128), depth)
     other = pl.ds(pl.multiple_of((1 - fsdp) * depth, 128), depth)
-    pairs = [
-        (tokens_ref.at[:, near], near_ref), (weight_ref, w), (target_ref, t), (tokens_ref.at[:, other], far_ref),
-    ]
+    cuts = [pl.ds(k, min(CUT, depth - k)) for k in range(0, depth, CUT)]
+    pairs = [(tokens_ref.at[:, near], near_ref)] + [(weight_ref.at[cut], w.at[cut]) for cut in cuts]
+    pairs += [(target_ref, t), (rights_ref, b_ref), (factor_ref, a_ref), (tokens_ref.at[:, other], far_ref)]
     copies = [pltpu.make_async_copy(s, d, sem.at[k]) for k, (s, d) in enumerate(pairs)]
     for c in copies:
         c.start()
-    for c in copies[:3]:
+    copies[0].wait()
+    for k, cut in enumerate(cuts):
+        copies[1 + k].wait()
+        part = jnp.dot(near_ref[:, cut], w[cut, :], preferred_element_type=f32)
+        if k + 1 == len(cuts):
+            copies[-4].wait()
+            part = part - t[...].astype(f32)
+        base_ref[...] = part if k == 0 else base_ref[...] + part
+    for c in copies[-3:]:
         c.wait()
-    base_ref[...] = jnp.dot(near_ref[...], w[...], preferred_element_type=f32) - t[...].astype(f32)
-    copies[3].wait()
-
-
-def near_half(tokens, weight, target):
+
+
+def near_half(tokens, weight, target, factor_a, factor_b):
     rows, width = target.shape
     depth = weight.shape[0]
     return pl.pallas_call(
         near_kernel,
-        in_specs=[hbm()] * 3,
-        out_specs=[vmem()] * 3,
+        in_specs=[hbm()] * 5,
+        out_specs=[vmem()] * 5,
         out_shape=[
             jax.ShapeDtypeStruct((rows, depth), bf16), jax.ShapeDtypeStruct((rows, depth), bf16),
-            jax.ShapeDtypeStruct((rows, width), f32),
+            jax.ShapeDtypeStruct((rows, width), f32), jax.ShapeDtypeStruct(factor_a.shape, bf16),
+            jax.ShapeDtypeStruct(factor_b.shape, bf16),
         ],
         scratch_shapes=[
-            pltpu.VMEM((depth, width), bf16), pltpu.VMEM((rows, width), bf16), pltpu.SemaphoreType.DMA((4,)),
+            pltpu.VMEM((depth, width), bf16), pltpu.VMEM((rows, width), bf16),
+            pltpu.SemaphoreType.DMA((5 + -(-depth // CUT),)),
         ],
         compiler_params=params(14),
         cost_estimate=pl.CostEstimate(flops=8 * rows * depth * width, bytes_accessed=8 << 20, transcendentals=0),
         name="near",
-    )(*in_hbm(tokens, weight, target))
+    )(*in_hbm(tokens, weight, target, factor_a, factor_b))
 
 
 def tables_kernel(
-    index_ref, counts_ref, near_ref, factor_ref, rights_ref,
-    sc_ref, hot_ref, few_ref, right_ref, columns_ref, chosen_ref, a, b, sem,
+    index_ref, counts_ref, near_ref, a, b, sc_ref, hot_ref, few_ref, right_ref, columns_ref, chosen_ref
 ):
     device = lax.axis_index("grp") * lax.axis_size("fsdp") + lax.axis_index("fsdp")
-    rows, pool = near_ref.shape[0], factor_ref.shape[1]
-    copies = [pltpu.make_async_copy(s, d, sem.at[k]) for k, (s, d) in enumerate([(rights_ref, b), (factor_ref, a)])]
-    for c in copies:
-        c.start()
+    rows, pool = near_ref.shape[0], a.shape[1]
     ends = ends_of(counts_ref)
     first = first_of(ends, device, rows)
     hot = owners(ends, counts_ref, device, rows)
     hot_ref[...] = hot
     few_ref[...] = few_of(hot, first)
-    copies[0].wait()
     chosen = lax.dot_general(
         matches(index_ref[1:2, :], pool), b[...], (((0,), (0,)), ((), ())), preferred_element_type=f32
     ).astype(bf16)
     chosen_ref[...] = chosen
     right_ref[...] = jnp.dot(hot, chosen, preferred_element_type=f32).astype(bf16)
-    copies[1].wait()
     columns_ref[...] = jnp.dot(a[...], matches(index_ref[0:1, :], pool), preferred_element_type=f32).astype(bf16)
     sc_ref[...] = across_dot(near_ref[...], batch_columns(index_ref[0:1, :], first, a[...]))
 
 
 def tables(index, counts, near, factor_a, factor_b):
     rows, depth = near.shape
-    (pool, width), cands = factor_b.shape, counts.shape[1]
+    width, cands = factor_b.shape[1], counts.shape[1]
 
     def shaped(*shape, dtype=bf16):
         return jax.ShapeDtypeStruct(shape, dtype)
 
     return pl.pallas_call(
         tables_kernel,
-        in_specs=[vmem()] * 3 + [hbm()] * 2,
+        in_specs=[vmem()] * 5,
         out_specs=[vmem()] * 6,
         out_shape=[
             shaped(rows, BATCH, dtype=f32), shaped(rows, cands), shaped(rows, BATCH, dtype=f32),
             shaped(rows, width), shaped(depth, cands), shaped(cands, width),
         ],
-        scratch_shapes=[
-            pltpu.VMEM((depth, pool), bf16), pltpu.VMEM((pool, width), bf16), pltpu.SemaphoreType.DMA((2,)),
-        ],
         compiler_params=params(12),
         cost_estimate=pl.CostEstimate(flops=8 * rows * depth * width, bytes_accessed=4 << 20, transcendentals=0),
         name="tables",
-    )(index, counts, near, *in_hbm(factor_a, factor_b))
+    )(index, counts, near, factor_a, factor_b)
 
 
 def stack(pieces, blocks, held):
@@ -412,8 +414,8 @@
         early, late = (
             [*some.values()] + [hop(v, 2, devices) for v in some.values()] for some in (early, late)
         )
-        near, far, base = near_half(tokens, weight, target)
-        sc, hot, few, right_rows, columns, chosen = tables(index, counts[None, :], near, factor_a, factor_b)
+        near, far, base, held_a, held_b = near_half(tokens, weight, target, factor_a, factor_b)
+        sc, hot, few, right_rows, columns, chosen = tables(index, counts[None, :], near, held_a, held_b)
         base, sc = middle(arrived, far, base, sc, taken, early)
         sums = losses(noise, arrived, far, base, sc, few, more, right_rows, hot, late, devices)
     else:

time: 75.8 us -> 74.9 us (0.988)
  Pallas kernels: 20.7 us -> 19.2 us
  local copies, waits for them, and re-layouts: 23.1 us -> 24.2 us
  waiting for transfers between devices: 2.61 us -> 1.8 us
    pallas_call x2, Pallas kernels: 7.97 us -> 6.44 us  [the longest x1 4 us: near_half(): pl.pallas_call(near_kernel, in_specs=[hbm()] * 5, out_specs=[vmem()] * 5,...]
    unnamed x64, local copies, waits for them, and re-layouts: 22.4 us -> 23.5 us
    ppermute x17, waiting for transfers between devices: 2.61 us -> 1.8 us  [hop(): return lax.ppermute(value, AXES, [(i, i ^ bit) for i in range(devices)])]
  transfers between devices with their start and end apart: 17 -> 17, of which waited for: 3 -> 2; matrix products, arithmetic and copies ran while one was open for 2% -> 2% of each run, Pallas kernels for 14% -> 12%
where the time goes in v4:
time: 74.9 us; the launch traced here: 74.3 us
  local copies, waits for them, and re-layouts  24.2 us (32%)
  Pallas kernels  19.2 us (26%)
  starting transfers between devices  14.9 us (20%)
  blocking collectives  11.8 us (16%)
  waiting for transfers between devices  1.8 us (2%)
  between operations  1.49 us (2%)
  other arithmetic  0.95 us (1%)
    unnamed x64, local copies, waits for them, and re-layouts  23.5 us
    ppermute x17, starting transfers between devices, hop(): return lax.ppermute(value, AXES, [(i, i ^ bit) for i in range(devices)])  14.9 us
    all_to_all x1, blocking collectives, compute(): spread = lax.all_to_all(sums, AXES, split_axis=0, concat_axis=0, tiled=True)  11.8 us
    pallas_call x1, Pallas kernels, update_of(): pl.pallas_call(functools.partial(update_kernel, step), in_specs=[vmem()]...  4.08 us
    pallas_call x1, Pallas kernels, near_half(): pl.pallas_call(near_kernel, in_specs=[hbm()] * 5, out_specs=[vmem()] * 5,...  4 us
    pallas_call x1, Pallas kernels, losses(): pl.pallas_call(functools.partial(loss_kernel, noise, order), in_specs=[vm...  2.98 us
    pallas_call x1, Pallas kernels, offer(): pl.pallas_call(functools.partial(offer_kernel, tokens), in_specs=[vmem(),...  2.86 us
    pallas_call x1, Pallas kernels, tables(): pl.pallas_call(tables_kernel, in_specs=[vmem()] * 5, out_specs=[vmem()] *...  2.44 us
  transfers between devices with their start and end apart: 17, of which 2 were waited for; matrix products, arithmetic and copies ran while one was open for 2% of the time, Pallas kernels for 12%

profile of v4, /device:TPU:0, one launch (start us, length us, event | category | flops | bytes accessed | tf_op | source)
XLA Modules:
  0.0 74.3 jit_solution(8791779195465803712)
XLA Ops:
  0.6 2.9 %offer.2 = bf16[32,1792]{1,0:T(8,128)(2,1)S(1)} custom-call(s32[2,256]{1,0:T(2,128)} %bitcast.6, s32[1,256]{1,0:T(1,128)} %bitcast.9, bf16[1792,512]{1,0:T(8,128)(2,1)} %factor_ref.3), custom_call_target="tpu_custom_call" | custom-call | tf_op jit(solution)/shard_map/offer/pallas_call | solution.py:79
  3.5 3.1 %collective-permute-start.1 = (bf16[32,1792]{1,0:T(8,128)(2,1)S(1)}, bf16[32,1792]{1,0:T(8,128)(2,1)S(1)}, u32[]{:S(2)}, u32[]{:S(2)}) collective-permute-start(bf16[32,1792]{1,0:T(8,128)(2,1)S(1)} %offer.2), channel_id=1, source_target_pairs={{0,1},{1,0},{2,3},{3,2},{4,5},{5,4},{6,7},{7,6},{8,9},{9,8},{10,11... | collective-permute-start | bytes 344072 | tf_op jit(solution)/shard_map/ppermute | solution.py:353
  6.6 1.3 %pack.1 = (bf16[112,1024]{1,0:T(8,128)(2,1)S(1)}, bf16[112,1024]{1,0:T(8,128)(2,1)S(1)}, bf16[112,1024]{1,0:T(8,128)(2,1)S(1)}, bf16[112,1024]{1,0:T(8,128)(2,1)S(1)}) custom-call(bf16[1792,1024]{1,0:T(8,128)(2,1)} %weight_ref.3), custom_call_target="tpu_custom_call" | custom-call | tf_op jit(solution)/shard_map/pack/pallas_call | solution.py:152
  8.0 2.0 %collective-permute-start.5 = (bf16[112,1024]{1,0:T(8,128)(2,1)S(1)}, bf16[112,1024]{1,0:T(8,128)(2,1)S(1)}, u32[]{:S(2)}, u32[]{:S(2)}) collective-permute-start(bf16[112,1024]{1,0:T(8,128)(2,1)S(1)} %get-tuple-element.66), channel_id=1, source_target_pairs={{0,1},{1,0},{2,3},{3,2},{4,5},{5,4},{6,7},{7,6},{8,9},{9,8},{10,11... | collective-permute-start | bytes 688136 | tf_op jit(solution)/shard_map/ppermute | solution.py:353
  10.1 4.0 %near.1 = (bf16[384,1792]{1,0:T(8,128)(2,1)S(1)}, bf16[384,1792]{1,0:T(8,128)(2,1)S(1)}, f32[384,1024]{1,0:T(8,128)S(1)}, bf16[1792,512]{1,0:T(8,128)(2,1)S(1)}, bf16[512,1024]{1,0:T(8,128)(2,1)S(1)}) custom-call(bf16[384,3584]{1,0:T(8,128)(2,1)} %tokens_ref.1, bf16[1792,1024]{1,0:T(8,128)(2,1)} %weight_ref.3, bf16[384,1024]{1,0:T(8,128)(2,1)} %target_ref.1, ...), custom_call_target="tpu_custom_call" | custom-call | flops 5637144576 | bytes 8388608 | tf_op jit(solution)/shard_map/near/pallas_call | solution.py:191
  14.1 1.1 %copy-done.26 = f32[384,1024]{1,0:T(8,128)} copy-done((f32[384,1024]{1,0:T(8,128)}, f32[384,1024]{1,0:T(8,128)S(1)}, u32[]{:S(2)}) %copy-start.26) | copy-done | bytes 1572888
  15.2 1.9 %collective-permute-start.13 = (bf16[112,1024]{1,0:T(8,128)(2,1)S(1)}, bf16[112,1024]{1,0:T(8,128)(2,1)}, u32[]{:S(2)}, u32[]{:S(2)}) collective-permute-start(bf16[112,1024]{1,0:T(8,128)(2,1)S(1)} %get-tuple-element.74), channel_id=1, source_target_pairs={{0,1},{1,0},{2,3},{3,2},{4,5},{5,4},{6,7},{7,6},{8,9},{9,8},{10,11... | collective-permute-start | bytes 688136 | tf_op jit(solution)/shard_map/ppermute | solution.py:353
  17.2 1.5 %collective-permute-start.3 = (bf16[112,1024]{1,0:T(8,128)(2,1)S(1)}, bf16[112,1024]{1,0:T(8,128)(2,1)S(1)}, u32[]{:S(2)}, u32[]{:S(2)}) collective-permute-start(bf16[112,1024]{1,0:T(8,128)(2,1)S(1)} %collective-permute-done.2.refs_0_), channel_id=1, source_target_pairs={{0,4},{1,5},{2,6},{3,7},{4,0},{5,1},{6,2},{7,3},{8,12},{9,13},{10,... | collective-permute-start | bytes 688136 | tf_op jit(solution)/shard_map/ppermute | solution.py:353
  18.7 1.6 %collective-permute-start.4 = (bf16[112,1024]{1,0:T(8,128)(2,1)S(1)}, bf16[112,1024]{1,0:T(8,128)(2,1)S(1)}, u32[]{:S(2)}, u32[]{:S(2)}) collective-permute-start(bf16[112,1024]{1,0:T(8,128)(2,1)S(1)} %collective-permute-done.2.refs_0_), channel_id=1, source_target_pairs={{0,8},{1,9},{2,10},{3,11},{4,12},{5,13},{6,14},{7,15},{8,0},{9,1},... | collective-permute-start | bytes 688136 | tf_op jit(solution)/shard_map/ppermute | solution.py:353
  20.2 1.1 %collective-permute-done.5.refs_3_ = bf16[112,1024]{1,0:T(8,128)(2,1)S(1)} collective-permute-done((bf16[112,1024]{1,0:T(8,128)(2,1)S(1)}, bf16[112,1024]{1,0:T(8,128)(2,1)S(1)}, u32[]{:S(2)}, u32[]{:S(2)}) %collective-permute-start.5) | collective-permute-done | bytes 229408 | tf_op jit(solution)/shard_map/ppermute | solution.py:353
  21.4 2.4 %tables.1 = (f32[384,32]{1,0:T(8,128)S(1)}, bf16[384,256]{1,0:T(8,128)(2,1)S(1)}, f32[384,32]{1,0:T(8,128)S(1)}, bf16[384,1024]{1,0:T(8,128)(2,1)S(1)}, bf16[179...) custom-call(s32[2,256]{1,0:T(2,128)S(1)} %bitcast.7, s32[1,256]{1,0:T(1,128)S(1)} %bitcast.10, ...), custom_call_target="tpu_custom_call" | custom-call | flops 5637144576 | bytes 4194304 | tf_op jit(solution)/shard_map/tables/pallas_call | solution.py:236
  28.5 1.5 %collective-permute-start.11 = (bf16[112,1024]{1,0:T(8,128)(2,1)S(1)}, bf16[112,1024]{1,0:T(8,128)(2,1)}, u32[]{:S(2)}, u32[]{:S(2)}) collective-permute-start(bf16[112,1024]{1,0:T(8,128)(2,1)S(1)} %collective-permute-done.10.refs_0_), channel_id=1, source_target_pairs={{0,4},{1,5},{2,6},{3,7},{4,0},{5,1},{6,2},{7,3},{8,12},{9,13},{10,... | collective-permute-start | bytes 688136 | tf_op jit(solution)/shard_map/ppermute | solution.py:353
  30.0 1.6 %collective-permute-start.12 = (bf16[112,1024]{1,0:T(8,128)(2,1)S(1)}, bf16[112,1024]{1,0:T(8,128)(2,1)}, u32[]{:S(2)}, u32[]{:S(2)}) collective-permute-start(bf16[112,1024]{1,0:T(8,128)(2,1)S(1)} %collective-permute-done.10.refs_0_), channel_id=1, source_target_pairs={{0,8},{1,9},{2,10},{3,11},{4,12},{5,13},{6,14},{7,15},{8,0},{9,1},... | collective-permute-start | bytes 688136 | tf_op jit(solution)/shard_map/ppermute | solution.py:353
  39.7 0.9 %copy-done.13 = bf16[112,1024]{1,0:T(8,128)(2,1)S(1)} copy-done((bf16[112,1024]{1,0:T(8,128)(2,1)S(1)}, bf16[112,1024]{1,0:T(8,128)(2,1)}, u32[]{:S(2)}) %copy-start.13) | copy-done | bytes 229400
  40.7 0.9 %copy-done.15 = bf16[112,1024]{1,0:T(8,128)(2,1)S(1)} copy-done((bf16[112,1024]{1,0:T(8,128)(2,1)S(1)}, bf16[112,1024]{1,0:T(8,128)(2,1)}, u32[]{:S(2)}) %copy-start.15) | copy-done | bytes 229400
  41.6 0.9 %copy-done.17 = bf16[112,1024]{1,0:T(8,128)(2,1)S(1)} copy-done((bf16[112,1024]{1,0:T(8,128)(2,1)S(1)}, bf16[112,1024]{1,0:T(8,128)(2,1)}, u32[]{:S(2)}) %copy-start.17) | copy-done | bytes 229400
  43.5 0.9 %copy-done.21 = bf16[112,1024]{1,0:T(8,128)(2,1)S(1)} copy-done((bf16[112,1024]{1,0:T(8,128)(2,1)S(1)}, bf16[112,1024]{1,0:T(8,128)(2,1)}, u32[]{:S(2)}) %copy-start.21) | copy-done | bytes 229400
  44.4 0.9 %copy-done.23 = bf16[112,1024]{1,0:T(8,128)(2,1)S(1)} copy-done((bf16[112,1024]{1,0:T(8,128)(2,1)S(1)}, bf16[112,1024]{1,0:T(8,128)(2,1)}, u32[]{:S(2)}) %copy-start.23) | copy-done | bytes 229400
  46.3 1.4 %copy-done.27 = f32[384,1024]{1,0:T(8,128)S(1)} copy-done((f32[384,1024]{1,0:T(8,128)S(1)}, f32[384,1024]{1,0:T(8,128)}, u32[]{:S(2)}) %copy-start.27) | copy-done | bytes 1572888
  48.6 1.5 %middle.1 = (f32[384,1024]{1,0:T(8,128)S(1)}, f32[384,32]{1,0:T(8,128)S(1)}) custom-call(bf16[384,1792]{1,0:T(8,128)(2,1)S(1)} %get-tuple-element.59.x_ref, f32[384,1024]{1,0:T(8,128)S(1)} %copy-done.27, f32[384,32]{1,0:T(8,128)S(1)} %copy-done.29, bf16[32,1792]{1,0:T(8,128)(2,1)S(1)} %collective-permute-done.1.cols_ref, ...), custom_call_target="tpu_custom_call" | custom-call | flops 2818572288 | bytes 4194304 | tf_op jit(solution)/shard_map/middle/pallas_call | solution.py:271
  51.5 1.1 %copy-done.3 = bf16[384,1024]{1,0:T(8,128)(2,1)S(1)} copy-done((bf16[384,1024]{1,0:T(8,128)(2,1)S(1)}, bf16[384,1024]{1,0:T(8,128)(2,1)}, u32[]{:S(2)}) %copy-start.3) | copy-done | bytes 786456
  55.4 3.0 %losses.1 = f32[32,1,256]{2,1,0:T(1,128)S(1)} custom-call(bf16[384,1792]{1,0:T(8,128)(2,1)S(1)} %get-tuple-element.59.x_ref, f32[384,1024]{1,0:T(8,128)S(1)} %get-tuple-element.67.base_ref, f32[384,32]{1,0:T(8,128)S(1)} %copy-done.11, f32[384,32]{1,0:T(8,128)S(1)} %copy-done.9, f32[384,1]{1,0:T(8,128)} %get-tuple-element.70.more_ref, ...), custom_call_target="tpu_custom_call" | custom-call | tf_op jit(solution)/shard_map/losses/pallas_call | solution.py:306
  58.4 11.8 %all_to_all.5.parts_ref = f32[32,1,256]{2,1,0:T(1,128)S(1)} all-to-all(f32[32,1,256]{2,1,0:T(1,128)S(1)} %losses.1), channel_id=1, replica_groups=mesh['grp'=16,'fsdp'=2] {'grp','fsdp'}, dimensions={0} | all-to-all | bytes 65536 | tf_op jit(solution)/shard_map/all_to_all | solution.py:439
  70.2 4.1 %update.1 = (f32[1792,1024]{1,0:T(8,128)}, f32[1,256]{1,0:T(1,128)}) custom-call(f32[32,1,256]{2,1,0:T(1,128)S(1)} %all_to_all.5.parts_ref, s32[1,256]{1,0:T(1,128)S(1)} %get-tuple-element.189, bf16[1792,256]{1,0:T(8,128)(2,1)S(1)} %copy-done.1, bf16[256,1024]{1,0:T(8,128)(2,1)S(1)} %copy-done.5), custom_call_target="tpu_custom_call" | custom-call | tf_op jit(solution)/shard_map/update/pallas_call | solution.py:341
  (89 shorter events, 19.3 us)
Async XLA Ops:
  3.5 15.2 %collective-permute-start.1 = (bf16[32,1792]{1,0:T(8,128)(2,1)S(1)}, bf16[32,1792]{1,0:T(8,128)(2,1)S(1)}, u32[]{:S(2)}, u32[]{:S(2)}) collective-permute-start(bf16[32,1792]{1,0:T(8,128)(2,1)S(1)} %offer.2), channel_id=1, source_target_pairs={{0,1},{1,0},{2,3},{3,2},{4,5},{5,4},{6,7},{7,6},{8,9},{9,8},{10,11... | collective-permute-start | bytes 344072 | tf_op jit(solution)/shard_map/ppermute | solution.py:353
  7.9 9.3 %collective-permute-start.2 = (bf16[112,1024]{1,0:T(8,128)(2,1)S(1)}, bf16[112,1024]{1,0:T(8,128)(2,1)S(1)}, u32[]{:S(2)}, u32[]{:S(2)}) collective-permute-start(bf16[112,1024]{1,0:T(8,128)(2,1)S(1)} %get-tuple-element.65), channel_id=1, source_target_pairs={{0,1},{1,0},{2,3},{3,2},{4,5},{5,4},{6,7},{7,6},{8,9},{9,8},{10,11... | collective-permute-start | bytes 688136 | tf_op jit(solution)/shard_map/ppermute | solution.py:353
  8.0 13.4 %collective-permute-start.5 = (bf16[112,1024]{1,0:T(8,128)(2,1)S(1)}, bf16[112,1024]{1,0:T(8,128)(2,1)S(1)}, u32[]{:S(2)}, u32[]{:S(2)}) collective-permute-start(bf16[112,1024]{1,0:T(8,128)(2,1)S(1)} %get-tuple-element.66), channel_id=1, source_target_pairs={{0,1},{1,0},{2,3},{3,2},{4,5},{5,4},{6,7},{7,6},{8,9},{9,8},{10,11... | collective-permute-start | bytes 688136 | tf_op jit(solution)/shard_map/ppermute | solution.py:353
  10.0 11.4 %copy-start.30 = (s32[256,2]{0,1:T(2,128)S(1)}, s32[256,2]{0,1:T(2,128)}, u32[]{:S(2)}) copy-start(s32[256,2]{0,1:T(2,128)} %param.15) | copy-start | bytes 6148
  10.0 11.4 %copy-start.31 = (s32[256]{0:T(256)S(1)}, s32[256]{0:T(256)}, u32[]{:S(2)}) copy-start(s32[256]{0:T(256)} %param.14) | copy-start | bytes 3076
  10.0 18.5 %collective-permute-start.10 = (bf16[112,1024]{1,0:T(8,128)(2,1)S(1)}, bf16[112,1024]{1,0:T(8,128)(2,1)S(1)}, u32[]{:S(2)}, u32[]{:S(2)}) collective-permute-start(bf16[112,1024]{1,0:T(8,128)(2,1)S(1)} %get-tuple-element.73), channel_id=1, source_target_pairs={{0,1},{1,0},{2,3},{3,2},{4,5},{5,4},{6,7},{7,6},{8,9},{9,8},{10,11... | collective-permute-start | bytes 688136 | tf_op jit(solution)/shard_map/ppermute | solution.py:353
  14.1 1.1 %copy-start.26 = (f32[384,1024]{1,0:T(8,128)}, f32[384,1024]{1,0:T(8,128)S(1)}, u32[]{:S(2)}) copy-start(f32[384,1024]{1,0:T(8,128)S(1)} %get-tuple-element.60.base_ref) | copy-start | bytes 4718596
  15.2 14.7 %collective-permute-start.13 = (bf16[112,1024]{1,0:T(8,128)(2,1)S(1)}, bf16[112,1024]{1,0:T(8,128)(2,1)}, u32[]{:S(2)}, u32[]{:S(2)}) collective-permute-start(bf16[112,1024]{1,0:T(8,128)(2,1)S(1)} %get-tuple-element.74), channel_id=1, source_target_pairs={{0,1},{1,0},{2,3},{3,2},{4,5},{5,4},{6,7},{7,6},{8,9},{9,8},{10,11... | collective-permute-start | bytes 688136 | tf_op jit(solution)/shard_map/ppermute | solution.py:353
  17.2 14.4 %collective-permute-start.3 = (bf16[112,1024]{1,0:T(8,128)(2,1)S(1)}, bf16[112,1024]{1,0:T(8,128)(2,1)S(1)}, u32[]{:S(2)}, u32[]{:S(2)}) collective-permute-start(bf16[112,1024]{1,0:T(8,128)(2,1)S(1)} %collective-permute-done.2.refs_0_), channel_id=1, source_target_pairs={{0,4},{1,5},{2,6},{3,7},{4,0},{5,1},{6,2},{7,3},{8,12},{9,13},{10,... | collective-permute-start | bytes 688136 | tf_op jit(solution)/shard_map/ppermute | solution.py:353
  18.7 12.9 %collective-permute-start.4 = (bf16[112,1024]{1,0:T(8,128)(2,1)S(1)}, bf16[112,1024]{1,0:T(8,128)(2,1)S(1)}, u32[]{:S(2)}, u32[]{:S(2)}) collective-permute-start(bf16[112,1024]{1,0:T(8,128)(2,1)S(1)} %collective-permute-done.2.refs_0_), channel_id=1, source_target_pairs={{0,8},{1,9},{2,10},{3,11},{4,12},{5,13},{6,14},{7,15},{8,0},{9,1},... | collective-permute-start | bytes 688136 | tf_op jit(solution)/shard_map/ppermute | solution.py:353
  21.3 10.2 %copy-start.12 = (bf16[112,1024]{1,0:T(8,128)(2,1)}, bf16[112,1024]{1,0:T(8,128)(2,1)S(1)}, u32[]{:S(2)}) copy-start(bf16[112,1024]{1,0:T(8,128)(2,1)S(1)} %collective-permute-done.5.refs_3_) | copy-start | bytes 688132
  21.3 11.4 %collective-permute-start.6 = (bf16[112,1024]{1,0:T(8,128)(2,1)S(1)}, bf16[112,1024]{1,0:T(8,128)(2,1)S(1)}, u32[]{:S(2)}, u32[]{:S(2)}) collective-permute-start(bf16[112,1024]{1,0:T(8,128)(2,1)S(1)} %collective-permute-done.2.refs_0_), channel_id=1, source_target_pairs={{0,2},{1,3},{2,0},{3,1},{4,6},{5,7},{6,4},{7,5},{8,10},{9,11},{10,... | collective-permute-start | bytes 688136 | tf_op jit(solution)/shard_map/ppermute | solution.py:353
  28.5 8.6 %collective-permute-start.11 = (bf16[112,1024]{1,0:T(8,128)(2,1)S(1)}, bf16[112,1024]{1,0:T(8,128)(2,1)}, u32[]{:S(2)}, u32[]{:S(2)}) collective-permute-start(bf16[112,1024]{1,0:T(8,128)(2,1)S(1)} %collective-permute-done.10.refs_0_), channel_id=1, source_target_pairs={{0,4},{1,5},{2,6},{3,7},{4,0},{5,1},{6,2},{7,3},{8,12},{9,13},{10,... | collective-permute-start | bytes 688136 | tf_op jit(solution)/shard_map/ppermute | solution.py:353
  30.0 7.8 %collective-permute-start.12 = (bf16[112,1024]{1,0:T(8,128)(2,1)S(1)}, bf16[112,1024]{1,0:T(8,128)(2,1)}, u32[]{:S(2)}, u32[]{:S(2)}) collective-permute-start(bf16[112,1024]{1,0:T(8,128)(2,1)S(1)} %collective-permute-done.10.refs_0_), channel_id=1, source_target_pairs={{0,8},{1,9},{2,10},{3,11},{4,12},{5,13},{6,14},{7,15},{8,0},{9,1},... | collective-permute-start | bytes 688136 | tf_op jit(solution)/shard_map/ppermute | solution.py:353
  31.5 4.4 %collective-permute-start.9 = (bf16[112,1024]{1,0:T(8,128)(2,1)S(1)}, bf16[112,1024]{1,0:T(8,128)(2,1)S(1)}, u32[]{:S(2)}, u32[]{:S(2)}) collective-permute-start(bf16[112,1024]{1,0:T(8,128)(2,1)S(1)} %collective-permute-done.5.refs_3_), channel_id=1, source_target_pairs={{0,2},{1,3},{2,0},{3,1},{4,6},{5,7},{6,4},{7,5},{8,10},{9,11},{10,... | collective-permute-start | bytes 688136 | tf_op jit(solution)/shard_map/ppermute | solution.py:353
  31.6 6.2 %collective-permute-start.7 = (bf16[112,1024]{1,0:T(8,128)(2,1)S(1)}, bf16[112,1024]{1,0:T(8,128)(2,1)S(1)}, u32[]{:S(2)}, u32[]{:S(2)}) collective-permute-start(bf16[112,1024]{1,0:T(8,128)(2,1)S(1)} %collective-permute-done.3.refs_1_), channel_id=1, source_target_pairs={{0,2},{1,3},{2,0},{3,1},{4,6},{5,7},{6,4},{7,5},{8,10},{9,11},{10,... | collective-permute-start | bytes 688136 | tf_op jit(solution)/shard_map/ppermute | solution.py:353
  33.5 5.5 %collective-permute-start.8 = (bf16[112,1024]{1,0:T(8,128)(2,1)S(1)}, bf16[112,1024]{1,0:T(8,128)(2,1)S(1)}, u32[]{:S(2)}, u32[]{:S(2)}) collective-permute-start(bf16[112,1024]{1,0:T(8,128)(2,1)S(1)} %collective-permute-done.4.refs_2_), channel_id=1, source_target_pairs={{0,2},{1,3},{2,0},{3,1},{4,6},{5,7},{6,4},{7,5},{8,10},{9,11},{10,... | collective-permute-start | bytes 688136 | tf_op jit(solution)/shard_map/ppermute | solution.py:353
  36.6 14.9 %collective-permute-start.14 = (bf16[112,1024]{1,0:T(8,128)(2,1)S(1)}, bf16[112,1024]{1,0:T(8,128)(2,1)}, u32[]{:S(2)}, u32[]{:S(2)}) collective-permute-start(bf16[112,1024]{1,0:T(8,128)(2,1)S(1)} %collective-permute-done.10.refs_0_), channel_id=1, source_target_pairs={{0,2},{1,3},{2,0},{3,1},{4,6},{5,7},{6,4},{7,5},{8,10},{9,11},{10,... | collective-permute-start | bytes 688136 | tf_op jit(solution)/shard_map/ppermute | solution.py:353
  37.0 14.5 %collective-permute-start.17 = (bf16[112,1024]{1,0:T(8,128)(2,1)}, bf16[112,1024]{1,0:T(8,128)(2,1)}, u32[]{:S(2)}, u32[]{:S(2)}) collective-permute-start(bf16[112,1024]{1,0:T(8,128)(2,1)} %collective-permute-done.13.refs_3_), channel_id=1, source_target_pairs={{0,2},{1,3},{2,0},{3,1},{4,6},{5,7},{6,4},{7,5},{8,10},{9,11},{10,... | collective-permute-start | bytes 688136 | tf_op jit(solution)/shard_map/ppermute | solution.py:353
  37.8 13.7 %collective-permute-start.15 = (bf16[112,1024]{1,0:T(8,128)(2,1)}, bf16[112,1024]{1,0:T(8,128)(2,1)}, u32[]{:S(2)}, u32[]{:S(2)}) collective-permute-start(bf16[112,1024]{1,0:T(8,128)(2,1)} %collective-permute-done.11.refs_1_), channel_id=1, source_target_pairs={{0,2},{1,3},{2,0},{3,1},{4,6},{5,7},{6,4},{7,5},{8,10},{9,11},{10,... | collective-permute-start | bytes 688136 | tf_op jit(solution)/shard_map/ppermute | solution.py:353
  38.5 13.0 %collective-permute-start.16 = (bf16[112,1024]{1,0:T(8,128)(2,1)}, bf16[112,1024]{1,0:T(8,128)(2,1)}, u32[]{:S(2)}, u32[]{:S(2)}) collective-permute-start(bf16[112,1024]{1,0:T(8,128)(2,1)} %collective-permute-done.12.refs_2_), channel_id=1, source_target_pairs={{0,2},{1,3},{2,0},{3,1},{4,6},{5,7},{6,4},{7,5},{8,10},{9,11},{10,... | collective-permute-start | bytes 688136 | tf_op jit(solution)/shard_map/ppermute | solution.py:353
  46.3 1.4 %copy-start.27 = (f32[384,1024]{1,0:T(8,128)S(1)}, f32[384,1024]{1,0:T(8,128)}, u32[]{:S(2)}) copy-start(f32[384,1024]{1,0:T(8,128)} %copy-done.26) | copy-start | bytes 4718596
  55.4 14.8 %copy-start.1 = (bf16[1792,256]{1,0:T(8,128)(2,1)S(1)}, bf16[1792,256]{1,0:T(8,128)(2,1)}, u32[]{:S(2)}) copy-start(bf16[1792,256]{1,0:T(8,128)(2,1)} %copy-done) | copy-start | bytes 2752516
  55.4 14.8 %copy-start.5 = (bf16[256,1024]{1,0:T(8,128)(2,1)S(1)}, bf16[256,1024]{1,0:T(8,128)(2,1)}, u32[]{:S(2)}) copy-start(bf16[256,1024]{1,0:T(8,128)(2,1)} %copy-done.4) | copy-start | bytes 1572868
  (25 other events, 21.0 us)
